TPU v7x, 32 devices: a whole 2x2x4 slice. The times are simulated.
32 devices in a mesh: dom: 8 (over y, x, core), slab: 4 (over z).
Axes of the slice: x: 2, y: 2, z: 4, core: 2. Of those that a mesh axis runs over, the one named last changes fastest.
Arguments:
- features: bfloat16 [4096, 128], P(('dom', 'slab')), may hold values from -6 to 6
- cotangent: bfloat16 [4096, 128], P(('dom', 'slab')), may hold values from -6 to 6
- positions: float32 [3, 4096], P(None, ('dom', 'slab')), may hold values from 0 to 1, as said below
- neighbours: int32 [16, 4096], P(None, ('dom', 'slab')), may hold values from 0 to 191
- counts: int32 [4096], P(('dom', 'slab')), may hold values from 4 to 16, as said below
- k_index: int32 [3, 2048], replicated, may hold values from -8 to 8, as said below
- k_filter: float32 [2048, 128], replicated, may hold values from -0.125 to 0.125
- w_radial: bfloat16 [16, 128], replicated, may hold values from -1.5 to 1.5
- w_out: bfloat16 [128, 128], replicated, may hold values from -0.5 to 0.5
Outputs:
- d_features: float32 [4096, 128], P(('dom', 'slab'))
- d_positions: float32 [3, 4096], P(None, ('dom', 'slab'))
- d_filter: float32 [2048, 128], P(('dom', 'slab'))
- d_radial: float32 [16, 128], replicated
- d_out: float32 [128, 128], replicated
Inputs may be any that keep to these rules, and one draw needn't show every extreme that they name: Atoms of domain (a, b) have positions[0] in [a / 8, (a + 1) / 8) and positions[1] in [b / 4, (b + 1) / 4). `neighbours`: entries index the domain's ghost buffer: its own 128 atoms, then 4 groups of 16 ghost atoms as the steps define. Slot s of atom i is live when s < counts[i]; the first atom of every domain uses all 16 slots. `k_index`: the 2048 vectors (columns) are distinct and non-zero, and no vector's negative is among them.
All inputs are finite; a program needn't handle non-finite values.
Results may differ from a plain program's by a relative error of at most 0.0054.
Values may be sent and summed in bfloat16 or wider, within the bound.
No kernel may reach another device: no remote copies, remote signals or barrier semaphores. Data moves between devices by JAX's collectives and lax.ppermute only.
A program may use at most 64 MiB of HBM per device.

v0:
```python
import functools
import math

import jax
import jax.numpy as jnp
from jax import lax
from jax.experimental import pallas as pl
from jax.experimental.pallas import tpu as pltpu
from jax.sharding import PartitionSpec as P


F32 = jnp.float32
BF16 = jnp.bfloat16
GROUP = 16
POS_ROWS = 16
MAGIC = 12582912.0
SIN_POLY = (
    6.28318528028833,
    -10.335420168095697,
    5.100155056857644,
    -1.196582599540606,
    0.15531532235506335,
)
COS_POLY = (
    0.9999999532943689,
    -4.934792832496617,
    4.058411371007551,
    -1.331876617475819,
    0.21968961468319229,
)


def horner(coefs, w):
    acc = jnp.full_like(w, coefs[-1])
    for c in coefs[-2::-1]:
        acc = acc * w + c
    return acc


def turn_trig(t):
    u = t - ((t + MAGIC) - MAGIC)
    w = u * u
    twice_sin = u * horner(SIN_POLY, w)
    half_cos = horner(COS_POLY, w)
    return 1.0 - 0.5 * twice_sin * twice_sin, twice_sin * half_cos


def three_pieces(value):
    high = value.astype(BF16)
    rest = value - high.astype(F32)
    mid = rest.astype(BF16)
    low = (rest - mid.astype(F32)).astype(BF16)
    return high, mid, low


def mm(first, second, dims):
    return lax.dot_general(first, second, (dims, ((), ())), preferred_element_type=F32)


NN = ((1,), (0,))
TN = ((0,), (0,))
NT = ((1,), (1,))


def packed(value):
    high, mid, low = (piece.astype(F32) for piece in three_pieces(value))
    return (high + pltpu.roll(mid, 3, 0)).astype(BF16), low.astype(BF16)


def place_rows(positions):
    zeros = jnp.zeros((5, positions.shape[1]), F32)
    first, second = packed(jnp.concatenate([positions, zeros], axis=0))
    return jnp.concatenate([first.astype(F32), second.astype(F32)], axis=0).astype(BF16)


def pos_of(rows, pieces=3):
    rows = rows.astype(F32)
    total = rows[0:8] + pltpu.roll(rows[0:8], 5, 0)
    return total + rows[8:16] if pieces == 3 else total


def pack_body(feat_hbm, cot_hbm, pos_hbm, own_ref, face_ref, pos_ref, sems):
    atoms = feat_hbm.shape[0]
    faces = 2 * (atoms // 8)
    copies = [
        pltpu.make_async_copy(pos_hbm, pos_ref, sems.at[0]),
        pltpu.make_async_copy(feat_hbm, own_ref.at[pl.ds(0, atoms)], sems.at[1]),
        pltpu.make_async_copy(cot_hbm, own_ref.at[pl.ds(atoms, atoms)], sems.at[2]),
    ]
    for copy in copies:
        copy.start()
    copies[0].wait()
    places = place_rows(pos_ref[...])
    own_ref[2 * atoms :, :] = places
    face_ref[faces:, :] = places
    copies[1].wait()
    face_ref[:faces, :] = own_ref[:faces]
    copies[2].wait()


def pack(features, cotangent, positions):
    atoms, channels = features.shape
    return pl.pallas_call(
        pack_body,
        out_shape=(
            jax.ShapeDtypeStruct((2 * atoms + POS_ROWS, channels), BF16),
            jax.ShapeDtypeStruct((2 * (atoms // 8) + POS_ROWS, channels), BF16),
        ),
        in_specs=[pl.BlockSpec(memory_space=pl.ANY)] * 3,
        scratch_shapes=[pltpu.VMEM((3, atoms), F32), pltpu.SemaphoreType.DMA((3,))],
        name="pack",
    )(features, cotangent, positions)


def structure_body(atoms, n_msg, has_partial, block, k_ref, *refs):
    msgs, refs = refs[:n_msg], refs[n_msg:]
    partial, refs = (refs[0], refs[1:]) if has_partial else (None, refs)
    cos_refs, sin_refs, out_refs = refs[:n_msg], refs[n_msg : 2 * n_msg], refs[2 * n_msg :]
    k_total = k_ref.shape[1]
    places = jnp.concatenate([m[2 * atoms :] for m in msgs], axis=1)
    values = jnp.concatenate(
        [jnp.concatenate([m[:atoms], m[atoms : 2 * atoms]], axis=1) for m in msgs], axis=0
    )
    rows = min(128, k_total)
    for j in range(k_total // rows):
        span = slice(j * rows, (j + 1) * rows)
        cosine, sine = turn_trig(mm(k_ref[:, span], places, TN))
        for i, (cos_ref, sin_ref) in enumerate(zip(cos_refs, sin_refs)):
            cos_ref[span, :] = cosine[:, i * atoms : (i + 1) * atoms]
            sin_ref[span, :] = sine[:, i * atoms : (i + 1) * atoms]
        re, im = mm(cosine.astype(BF16), values, NN), mm(sine.astype(BF16), values, NN)
        width = re.shape[1]
        if has_partial:
            re = re + partial[span, :width]
            im = im + partial[span, width:]
        if len(out_refs) == 1:
            out_refs[0][span, :width] = re
            out_refs[0][span, width:] = im
            continue
        for at in range(span.start // block, span.stop // block):
            part = slice(at * block - span.start, (at + 1) * block - span.start)
            out_refs[at][:, :width] = re[part].astype(out_refs[at].dtype)
            out_refs[at][:, width:] = im[part].astype(out_refs[at].dtype)


def structure(k_rows, msgs, atoms, channels, partial=None, chips=1):
    k_total = k_rows.shape[1]
    n = len(msgs)
    block = k_total // chips
    tables = (jax.ShapeDtypeStruct((k_total, atoms), F32),) * (2 * n)
    sums = (jax.ShapeDtypeStruct((block, 4 * channels), F32),)
    sums += (jax.ShapeDtypeStruct((block, 4 * channels), BF16),) * (chips - 1)
    operands = (k_rows, *msgs) + (() if partial is None else (partial,))
    outs = pl.pallas_call(
        functools.partial(structure_body, atoms, n, partial is not None, block),
        out_shape=tables + sums,
        compiler_params=pltpu.CompilerParams(vmem_limit_bytes=8 * 2**20),
        cost_estimate=pl.CostEstimate(
            flops=1_000_000_000 * n, bytes_accessed=1_000_000 * n, transcendentals=0
        ),
    )(*operands)
    return outs[:n], outs[n : 2 * n], outs[2 * n :]


def extra_rows(grad_rows, face):
    return -(-max(-(-grad_rows // 3), face + 16) // 16) * 16


def shares_body(scale, own_ref, filter_ref, extra_ref, *refs):
    others, (total_ref, share_ref) = refs[:-2], refs[-2:]
    total = own_ref[...]
    for other in others:
        total = total + other[...].astype(F32)
    total = scale * total
    total_ref[...] = total
    extra = extra_ref.shape[0]
    share_ref[:extra, :] = extra_ref[...]
    share_ref[extra:, :] = (jnp.concatenate([filter_ref[...]] * 4, axis=1) * total).astype(BF16)


def make_shares(scale, own, k_filter, extra, others):
    return pl.pallas_call(
        functools.partial(shares_body, scale),
        out_shape=(
            jax.ShapeDtypeStruct(own.shape, F32),
            jax.ShapeDtypeStruct((extra.shape[0] + own.shape[0], own.shape[1]), BF16),
        ),
        compiler_params=pltpu.CompilerParams(vmem_limit_bytes=8 * 2**20),
        cost_estimate=pl.CostEstimate(
            flops=200_000_000, bytes_accessed=600_000, transcendentals=0
        ),
        name="shares",
    )(own, k_filter, extra, *others)


def half_backward(atoms, pos_unit, msgs, k_ref, cos_refs, sin_refs, shares, extra):
    c = shares[0].shape[1] // 4
    share = jnp.concatenate([s[extra:] for s in shares], axis=0)
    source = jnp.concatenate(
        [
            jnp.concatenate([m[atoms : 2 * atoms], m[:atoms]], axis=1)
            for m in (ref[...] for ref in msgs)
        ],
        axis=0,
    )
    cosine = jnp.concatenate([ref[...] for ref in cos_refs], axis=1)
    sine = jnp.concatenate([ref[...] for ref in sin_refs], axis=1)
    feat = mm(share[:, c : 2 * c], cosine.astype(BF16), TN) + mm(
        share[:, 3 * c :], sine.astype(BF16), TN
    )
    p = mm(share[:, : 2 * c], source, NT)
    q = mm(share[:, 2 * c :], source, NT)
    weight = cosine * q - sine * p
    high = weight.astype(BF16)
    low = (weight - high.astype(F32)).astype(BF16)
    k16 = k_ref[...]
    place = (mm(k16, high, NN) + mm(k16, low, NN))[0:8]
    row = lax.broadcasted_iota(jnp.int32, place.shape, 0)
    return feat, jnp.where(row < 3, pos_unit * place, 0.0)


def group_rows(value, face, atoms, group):
    c = value.shape[1]
    above, below = group * face, atoms - (group + 1) * face
    pieces = [jnp.zeros((above, c), F32)] if above else []
    return jnp.concatenate(pieces + [value, jnp.zeros((below, c), F32)], axis=0)


def group_lanes(value, face, source, group):
    atoms = value.shape[1]
    lane = lax.broadcasted_iota(jnp.int32, value.shape, 1)
    turned = pltpu.roll(value, ((group - source) * face) % atoms, 1)
    return jnp.where((lane >= group * face) & (lane < (group + 1) * face), turned, 0.0)


def back_other_body(atoms, n_msg, n_share, pos_unit, extra, where_ref, k_ref, *refs):
    cos_refs, sin_refs, msgs = refs[:n_msg], refs[n_msg : 2 * n_msg], refs[2 * n_msg : 3 * n_msg]
    refs = refs[3 * n_msg :]
    shares, refs = refs[:n_share], refs[n_share:]
    buf_ref, move_ref, grad0_ref, sum_ref = refs
    c = buf_ref.shape[1]
    face = atoms // 8
    grad = grad0_ref[...]
    passed = jnp.zeros((face, c), F32)
    passed_moves = jnp.zeros((8, atoms), F32)
    for j, ref in enumerate(shares):
        if j:
            parts = [ref[:extra, i * c : (i + 1) * c].astype(F32) for i in range(3)]
            grad = grad + jnp.concatenate(parts, axis=0)[: grad.shape[0]]
        backs = ref[: face + 16, 3 * c :].astype(F32)
        sel = where_ref[2 + j : 3 + j]
        passed = passed + sel * backs[:face]
        tile = backs[face : face + 8]
        passed_moves = passed_moves + sel * (tile + pltpu.roll(tile, 5, 0) + backs[face + 8 :])
    even, odd = where_ref[0:1], where_ref[1:2]
    ghost_0, ghost_1 = buf_ref[atoms : atoms + face], buf_ref[atoms + face : atoms + 2 * face]
    rows_0 = even * ghost_1 + odd * passed
    rows_1 = even * passed + odd * ghost_0
    ours = move_ref[:, atoms:]
    moves = group_lanes(even * ours + odd * passed_moves, face, 1, 0) + group_lanes(
        even * passed_moves + odd * ours, face, 0, 1
    )
    feat, place = half_backward(
        atoms, pos_unit, msgs, k_ref, cos_refs, sin_refs, shares, extra
    )
    for d in range(n_msg):
        rows = feat[:, d * atoms : (d + 1) * atoms].T
        spots = place[:, d * atoms : (d + 1) * atoms]
        if d == 0:
            top = jnp.concatenate([rows_0, rows_1], axis=0)
            rows = jnp.concatenate([rows[: 2 * face] + top, rows[2 * face :]], axis=0)
            spots = spots + moves
        sum_ref[d * atoms : (d + 1) * atoms, :] = rows
        first = n_msg * atoms + d * 8
        sum_ref[first : first + 8, :] = spots
    sum_ref[n_msg * (atoms + 8) :, :] = grad


def back_own_body(atoms, n_msg, n_share, pos_unit, extra, k_ref, *refs):
    cos_refs, sin_refs, msgs = refs[:n_msg], refs[n_msg : 2 * n_msg], refs[2 * n_msg : 3 * n_msg]
    refs = refs[3 * n_msg :]
    shares, refs = refs[:n_share], refs[n_share:]
    buf_ref, move_ref, sum_ref = refs
    face = atoms // 8
    feat, place = half_backward(
        atoms, pos_unit, msgs, k_ref, cos_refs, sin_refs, shares, extra
    )
    ghost_move = move_ref[:, atoms:]
    for d in range(n_msg):
        rows = feat[:, d * atoms : (d + 1) * atoms].T
        spots = place[:, d * atoms : (d + 1) * atoms]
        if d == 0:
            rows = rows + buf_ref[:atoms]
            spots = spots + move_ref[:, :atoms]
        for shift, ghost, group in ((1, 2, 3), (n_msg - 1, 3, 2)):
            if d == shift:
                part = buf_ref[atoms + ghost * face : atoms + (ghost + 1) * face]
                rows = rows + group_rows(part, face, atoms, group)
                spots = spots + group_lanes(ghost_move, face, ghost, group)
        sum_ref[d * atoms : (d + 1) * atoms, :] = rows
        first = n_msg * atoms + d * 8
        sum_ref[first : first + 8, :] = spots


def join_body(atoms, n_msg, here_ref, there_ref, sent_ref, own_ref, *out_refs):
    tail = n_msg * (atoms + 8)
    row = lax.broadcasted_iota(jnp.int32, (8, atoms), 0)
    grad = sent_ref[tail:] + there_ref[tail:]
    own_ref[atoms + 8 :, :] = grad
    grad = grad.astype(BF16)
    for d in range(n_msg):
        span = slice(d * atoms, (d + 1) * atoms)
        spot = slice(n_msg * atoms + d * 8, n_msg * atoms + d * 8 + 8)
        rows = here_ref[span] + sent_ref[span]
        spots = here_ref[spot] + sent_ref[spot]
        if d == 0:
            own_ref[:atoms, :] = rows
            own_ref[atoms : atoms + 8, :] = spots
            continue
        out = out_refs[d - 1]
        out[:atoms, :] = rows.astype(BF16)
        spots = jnp.where(row < 3, spots, 0.0)
        out[atoms : atoms + POS_ROWS, :] = jnp.concatenate(packed(spots), axis=0)
        out[atoms + POS_ROWS :, :] = grad


def back_call(body, out_shape, *operands):
    return pl.pallas_call(
        body,
        out_shape=out_shape,
        compiler_params=pltpu.CompilerParams(vmem_limit_bytes=8 * 2**20),
        cost_estimate=pl.CostEstimate(
            flops=3_000_000_000, bytes_accessed=4_000_000, transcendentals=0
        ),
    )(*operands)


def pair_body(
    atoms,
    channels,
    group,
    pos_unit,
    where_ref,
    own_ref,
    flip_ref,
    cross_ref,
    below_ref,
    above_ref,
    nbr_ref,
    count_ref,
    wr_ref,
    wo_ref,
    buf_out,
    move_out,
    grad_out,
    extra_ref,
    buf_acc,
    mat_ref,
):
    slots = nbr_ref.shape[0]
    levels, hidden = wr_ref.shape
    face = atoms // 8
    wide = 2 * atoms
    span = group * atoms
    f32_of = lambda rows: rows.astype(F32)
    even, odd = where_ref[0:1], where_ref[1:2]
    cross = f32_of(cross_ref[...])
    flip_faces, flip_spots = f32_of(flip_ref[: 2 * face]), f32_of(flip_ref[2 * atoms :])
    below = odd * flip_faces + even * cross[: 2 * face]
    above = even * flip_faces + odd * cross[: 2 * face]
    ghosts = (
        (below[face:], odd * flip_spots + even * cross[2 * face :], 1),
        (above[:face], even * flip_spots + odd * cross[2 * face :], 0),
        (f32_of(below_ref[3 * face : 4 * face]), f32_of(below_ref[2 * atoms :]), 3),
        (f32_of(above_ref[2 * face : 3 * face]), f32_of(above_ref[2 * atoms :]), 2),
    )
    lane = lax.broadcasted_iota(jnp.int32, (POS_ROWS, atoms), 1)
    ghost = jnp.zeros((POS_ROWS, atoms), F32)
    for slot, (_, spot, source) in enumerate(ghosts):
        turned = pltpu.roll(spot, ((slot - source) * face) % atoms, 1)
        inside = (lane >= slot * face) & (lane < (slot + 1) * face)
        ghost = jnp.where(inside, turned, ghost)
    own_rows = own_ref[2 * atoms :]
    places = jnp.concatenate([own_rows, ghost.astype(BF16)], axis=1)
    rows = [f32_of(own_ref[:atoms])] + [g[0] for g in ghosts]
    rows.append(jnp.zeros((wide - atoms - 4 * face, channels), F32))
    features_t = jnp.concatenate(rows, axis=0).T.astype(BF16)
    mat_ref[:channels, :] = features_t
    mat_ref[channels:, :] = places
    cot_t = f32_of(own_ref[atoms : 2 * atoms]).T * (1.0 / math.sqrt(slots))
    source_pos = pos_of(own_rows)
    source_pos = jnp.concatenate([source_pos] * group, axis=1)
    cot_rep = jnp.concatenate([cot_t] * group, axis=1)
    steps = lax.broadcasted_iota(jnp.int32, (levels, span), 0).astype(F32)
    rates = 0.5 * jnp.exp(steps * (math.log(16.0) / (levels - 1)))
    buffer_row = lax.broadcasted_iota(jnp.int32, (wide, span), 0)
    axis = lax.broadcasted_iota(jnp.int32, (8, span), 0)
    w_radial = wr_ref[...]
    w_out = wo_ref[...]
    buf_acc[...] = jnp.zeros_like(buf_acc)
    grad_out[...] = jnp.zeros_like(grad_out)
    move_out[...] = jnp.zeros_like(move_out)

    def step(g, carry):
        index = jnp.concatenate([nbr_ref[pl.ds(g * group + s, 1), :] for s in range(group)], axis=1)
        live = jnp.concatenate(
            [jnp.where(count_ref[...] > g * group + s, 1.0, 0.0) for s in range(group)], axis=1
        )
        picked = jnp.where(buffer_row == index, 1.0, 0.0).astype(BF16)
        taken = mm(mat_ref[...], picked, NN)
        feat = taken[:channels]
        offset = jnp.where(axis < 3, pos_of(taken[channels:]) - source_pos, 0.0)
        cosine, chord = turn_trig(offset)
        dist2 = jnp.sum(chord * chord, axis=0, keepdims=True)
        rbf = jnp.exp(-rates * dist2)
        rbf_h = rbf.astype(BF16)
        pre = mm(w_radial, rbf_h, TN)
        gate = jax.nn.sigmoid(pre)
        act = (pre * gate).astype(BF16)
        phi = mm(w_out, act, TN)
        weight = cot_rep * live
        message = weight * phi
        high = message.astype(BF16)
        low = (message - high.astype(F32)).astype(BF16)
        buf_acc[...] += mm(picked, high, NT) + mm(picked, low, NT)
        dphi = (weight * feat).astype(BF16)
        grad_out[levels:, :] += mm(act, dphi, NT)
        d_act = mm(w_out, dphi, NN)
        dpre = (d_act * gate * (1.0 + pre * (1.0 - gate))).astype(BF16)
        grad_out[:levels, :] += mm(rbf_h, dpre, NT)
        d_rbf = mm(w_radial, dpre, NN)
        d_chord2 = -jnp.sum(d_rbf * rates * rbf, axis=0, keepdims=True)
        dmove = (2.0 * pos_unit) * d_chord2 * chord * cosine
        pieces = jnp.concatenate([v.astype(F32) for v in three_pieces(dmove)], axis=0).astype(BF16)
        moved = mm(pieces, picked, NT)
        move_out[...] += moved[0:8] + moved[8:16] + moved[16:24]
        back = dmove[:, :atoms]
        for s in range(1, group):
            back = back + dmove[:, s * atoms : (s + 1) * atoms]
        move_out[:, :atoms] -= back
        return carry

    lax.fori_loop(0, slots // group, step, 0)
    buf_out[...] = buf_acc[: atoms + 4 * face]
    extra = extra_ref.shape[0]
    for j in range(3):
        part = grad_out[j * extra : min((j + 1) * extra, levels + hidden)]
        extra_ref[: part.shape[0], j * channels : (j + 1) * channels] = part.astype(BF16)
    places = jnp.concatenate([f32_of(v) for v in packed(move_out[:, atoms:])], axis=0)
    group_0, group_1 = buf_acc[atoms : atoms + face], buf_acc[atoms + face : atoms + 2 * face]
    extra_ref[:face, 3 * channels :] = (even * group_0 + odd * group_1).astype(BF16)
    extra_ref[face : face + 16, 3 * channels :] = places.astype(BF16)


def pair_part(where, sources, neighbours, counts, w_radial, w_out, pos_unit):
    _, atoms = neighbours.shape
    levels, hidden = w_radial.shape
    channels = w_out.shape[1]
    face = atoms // 8
    group = GROUP
    return pl.pallas_call(
        functools.partial(pair_body, atoms, channels, group, pos_unit),
        out_shape=(
            jax.ShapeDtypeStruct((atoms + 4 * face, channels), F32),
            jax.ShapeDtypeStruct((8, 2 * atoms), F32),
            jax.ShapeDtypeStruct((levels + hidden, channels), F32),
            jax.ShapeDtypeStruct((extra_rows(levels + hidden, face), 4 * channels), BF16),
        ),
        scratch_shapes=[
            pltpu.VMEM((2 * atoms, channels), F32),
            pltpu.VMEM((channels + POS_ROWS, 2 * atoms), BF16),
        ],
        compiler_params=pltpu.CompilerParams(vmem_limit_bytes=12 * 2**20),
        cost_estimate=pl.CostEstimate(
            flops=4_000_000_000, bytes_accessed=1_000_000, transcendentals=500_000
        ),
        name="pairs",
    )(where, *sources, neighbours, counts.reshape(1, atoms), w_radial, w_out)


def finish_body(atoms, n_msg, scale, own_ref, total_ref, *refs):
    msgs, (feat_ref, pos_ref, filter_ref, radial_ref, out_ref) = refs[:n_msg], refs[n_msg:]
    feat, place, grad = own_ref[:atoms], own_ref[atoms : atoms + 8], own_ref[atoms + 8 :]
    for m in msgs:
        feat = feat + m[:atoms].astype(F32)
        place = place + pos_of(m[atoms : atoms + POS_ROWS])
        grad = grad + m[atoms + POS_ROWS :].astype(F32)
    levels = radial_ref.shape[0]
    c = feat_ref.shape[1]
    re = total_ref[:, :c] * total_ref[:, c : 2 * c]
    filter_ref[...] = re + total_ref[:, 2 * c : 3 * c] * total_ref[:, 3 * c :]
    feat_ref[...] = feat
    pos_ref[...] = place[0:3]
    radial_ref[...] = scale * grad[:levels]
    out_ref[...] = scale * grad[levels:]


def finish(scale, atoms, levels, own, total, msgs):
    channels = own.shape[1]
    return pl.pallas_call(
        functools.partial(finish_body, atoms, len(msgs), scale),
        out_shape=(
            jax.ShapeDtypeStruct((atoms, channels), F32),
            jax.ShapeDtypeStruct((3, atoms), F32),
            jax.ShapeDtypeStruct((total.shape[0], channels), F32),
            jax.ShapeDtypeStruct((levels, channels), F32),
            jax.ShapeDtypeStruct((own.shape[0] - atoms - 8 - levels, channels), F32),
        ),
        compiler_params=pltpu.CompilerParams(vmem_limit_bytes=8 * 2**20),
        name="finish",
    )(own, total, *msgs)


def along(block, axis, shift):
    n = lax.axis_size(axis)
    return lax.ppermute(block, axis, [((i - shift) % n, i) for i in range(n)])


def swapped(block, axis, mask):
    n = lax.axis_size(axis)
    return lax.ppermute(block, axis, [(i, i ^ mask) for i in range(n)])


def bits_of(n):
    return [1 << b for b in range(n.bit_length() - 1)]


def reordered(values, index, axis):
    n = values.shape[axis]
    for bit in bits_of(n):
        shape = values.shape[:axis] + (n // (2 * bit), 2, bit) + values.shape[axis + 1 :]
        split = values.reshape(shape)
        turned = jnp.flip(split, axis + 1)
        values = jnp.where((index & bit) > 0, turned, split).reshape(values.shape)
    return values


def program(features, cotangent, positions, neighbours, counts, k_index, k_filter, w_radial, w_out):
    atoms, channels = features.shape
    n_dom, n_slab = lax.axis_size("dom"), lax.axis_size("slab")
    devices = n_dom * n_slab
    chips = n_dom // 2
    scale = 1.0 / math.sqrt(atoms * devices)
    k_total = k_index.shape[1]
    pos_unit = 1.0 / math.sqrt(k_total)
    block = k_total // devices
    dom, slab = lax.axis_index("dom"), lax.axis_index("slab")

    own, faces = pack(features, cotangent, positions)
    msgs = [own]
    for d in range(1, n_slab):
        msgs.append(along(own, "slab", d))
    across = [(i, (i + 1 if i % 2 else i - 1) % n_dom) for i in range(n_dom)]
    cross = lax.ppermute(faces, "dom", across)
    others = [swapped(own, "dom", 1)]

    core, chip = dom & 1, dom >> 1
    k_own = k_index.reshape(3, chips, 2 * n_slab, block)
    k_own = lax.dynamic_index_in_dim(k_own, core * n_slab + slab, 2, False)
    k_own = reordered(k_own, chip, 1).reshape(3, chips * block)
    k_own = k_own.astype(BF16)
    gap = jnp.zeros((5, chips * block), BF16)
    k_rows = jnp.concatenate([k_own, k_own, gap[:2], k_own, gap], axis=0)
    filter_rows = lax.dynamic_slice_in_dim(k_filter, (dom * n_slab + slab) * block, block, 0)
    across_of = ((dom ^ 1) + jnp.where(core == 0, 1, n_dom - 1)) % n_dom
    row = lax.broadcasted_iota(jnp.int32, (-(-(2 + chips) // 8) * 8, channels), 0)
    where = ((row == core) | (row == 2 + ((across_of >> 1) ^ chip))).astype(F32)
    own, k_rows, filter_rows, where = lax.optimization_barrier(
        (own, k_rows, filter_rows, where)
    )
    msgs[0] = own

    far = n_slab // 2
    near = [d for d in range(1, n_slab) if d != far]
    cos_e, sin_e, sums = structure(k_rows, (own, others[0]), atoms, channels)
    tables = {0: (cos_e, sin_e)}
    others = others + [None] * (n_slab - 1)
    for d in near:
        msgs[d], sums = lax.optimization_barrier((msgs[d], sums))
        others[d] = swapped(msgs[d], "dom", 1)
    if near:
        taken = [msgs[d] for d in near] + [others[d] for d in near]
        cos_n, sin_n, sums = structure(k_rows, taken, atoms, channels, *sums)
        for i, d in enumerate(near):
            both = (i, i + len(near))
            tables[d] = tuple([table[j] for j in both] for table in (cos_n, sin_n))
    others[far] = swapped(msgs[far], "dom", 1)
    cos_l, sin_l, sums = structure(
        k_rows, (msgs[far], others[far]), atoms, channels, *sums, chips=chips
    )
    tables[far] = (cos_l, sin_l)
    tables_own, tables_other = (
        [tables[d][part][core_of] for part in range(2) for d in range(n_slab)]
        for core_of in range(2)
    )
    s_own, *pieces = sums
    arrived = [swapped(piece, "dom", 2 * s) for s, piece in enumerate(pieces, 1)]

    cross, pieces = lax.optimization_barrier((cross, pieces))
    sources = (msgs[0], others[0], cross, msgs[1], msgs[-1])
    buf, moves, grads, riders = pair_part(
        where, sources, neighbours, counts, w_radial, w_out, pos_unit
    )
    total, share = make_shares(scale, s_own, filter_rows, riders, arrived)
    shares = [share] + [swapped(share, "dom", 2 * s) for s in range(1, chips)]

    extra = share.shape[0] - block
    settings = (atoms, n_slab, len(shares), pos_unit, extra)
    rows = n_slab * (atoms + 8)
    there = back_call(
        functools.partial(back_other_body, *settings),
        jax.ShapeDtypeStruct((rows + grads.shape[0], channels), F32),
        where,
        k_rows,
        *tables_other,
        *others,
        *shares,
        buf,
        moves,
        grads,
    )
    sent = swapped(there, "dom", 1)
    here = back_call(
        functools.partial(back_own_body, *settings),
        jax.ShapeDtypeStruct((rows, channels), F32),
        k_rows,
        *tables_own,
        *msgs,
        *shares,
        buf,
        moves,
    )
    message = jax.ShapeDtypeStruct((atoms + POS_ROWS + grads.shape[0], channels), BF16)
    own_sum, *partials = back_call(
        functools.partial(join_body, atoms, n_slab),
        (jax.ShapeDtypeStruct((atoms + 8 + grads.shape[0], channels), F32),)
        + (message,) * (n_slab - 1),
        here,
        there,
        sent,
    )
    returned = [along(partials[d - 1], "slab", -d) for d in [far] + near]
    return finish(scale, atoms, w_radial.shape[0], own_sum, total, returned)


def solution(mesh):
    in_specs = (
        P(("dom", "slab"), None),
        P(("dom", "slab"), None),
        P(None, ("dom", "slab")),
        P(None, ("dom", "slab")),
        P(("dom", "slab")),
        P(),
        P(),
        P(),
        P(),
    )
    out_specs = (
        P(("dom", "slab"), None),
        P(None, ("dom", "slab")),
        P(("dom", "slab"), None),
        P(),
        P(),
    )
    return jax.shard_map(program, mesh=mesh, in_specs=in_specs, out_specs=out_specs, check_vma=False)
```

profile of v0, /device:TPU:0, one launch (start us, length us, event | category | flops | bytes accessed | tf_op | source)
XLA Modules:
  0.0 45.3 jit_solution(11330579436501001759)
XLA Ops:
  0.6 1.5 %pack.1 = (bf16[272,128]{1,0:T(8,128)(2,1)}, bf16[48,128]{1,0:T(8,128)(2,1)}) custom-call(bf16[128,128]{1,0:T(8,128)(2,1)} %feat_hbm.1, bf16[128,128]{1,0:T(8,128)(2,1)} %cot_hbm.1, f32[3,128]{1,0:T(4,128)} %pos_hbm.1), custom_call_target="tpu_custom_call" | custom-call | tf_op jit(solution)/shard_map/pack/pallas_call | solution.py:103
  2.2 0.6 %collective-permute-start = (bf16[272,128]{1,0:T(8,128)(2,1)}, bf16[272,128]{1,0:T(8,128)(2,1)S(1)}, u32[]{:S(2)}, u32[]{:S(2)}) collective-permute-start(bf16[272,128]{1,0:T(8,128)(2,1)} %get-tuple-element.50.refs_0_.own_ref.refs_8_), channel_id=1, source_target_pairs={{0,4},{4,0},{8,12},{12,8},{16,20},{20,16},{24,28},{28,24},{1,5},{5... | collective-permute-start | bytes 208904 | tf_op jit(solution)/shard_map/ppermute | solution.py:521
  2.8 2.6 %collective-permute-start.1 = (bf16[272,128]{1,0:T(8,128)(2,1)}, bf16[272,128]{1,0:T(8,128)(2,1)S(1)}, u32[]{:S(2)}, u32[]{:S(2)}) collective-permute-start(bf16[272,128]{1,0:T(8,128)(2,1)} %get-tuple-element.50.refs_0_.own_ref.refs_8_), channel_id=1, source_target_pairs={{3,0},{0,1},{1,2},{2,3},{7,4},{4,5},{5,6},{6,7},{11,8},{8,9},{9,10... | collective-permute-start | bytes 208904 | tf_op jit(solution)/shard_map/ppermute | solution.py:516
  5.4 2.1 %collective-permute-start.2 = (bf16[272,128]{1,0:T(8,128)(2,1)}, bf16[272,128]{1,0:T(8,128)(2,1)S(1)}, u32[]{:S(2)}, u32[]{:S(2)}) collective-permute-start(bf16[272,128]{1,0:T(8,128)(2,1)} %get-tuple-element.50.refs_0_.own_ref.refs_8_), channel_id=1, source_target_pairs={{1,0},{2,1},{3,2},{0,3},{5,4},{6,5},{7,6},{4,7},{9,8},{10,9},{11,1... | collective-permute-start | bytes 208904 | tf_op jit(solution)/shard_map/ppermute | solution.py:516
  7.5 0.9 %collective-permute-start.5 = (bf16[272,128]{1,0:T(8,128)(2,1)}, bf16[272,128]{1,0:T(8,128)(2,1)S(1)}, u32[]{:S(2)}, u32[]{:S(2)}) collective-permute-start(bf16[272,128]{1,0:T(8,128)(2,1)} %get-tuple-element.50.refs_0_.own_ref.refs_8_), channel_id=1, source_target_pairs={{2,0},{3,1},{0,2},{1,3},{6,4},{7,5},{4,6},{5,7},{10,8},{11,9},{8,1... | collective-permute-start | bytes 208904 | tf_op jit(solution)/shard_map/ppermute | solution.py:516
  8.9 0.6 %copy-done.1 = bf16[272,128]{1,0:T(8,128)(2,1)S(1)} copy-done((bf16[272,128]{1,0:T(8,128)(2,1)S(1)}, bf16[272,128]{1,0:T(8,128)(2,1)}, u32[]{:S(2)}) %copy-start.1) | copy-done | bytes 69656
  9.5 0.6 %shard_map.128 = (f32[256,128]{1,0:T(8,128)S(1)}, f32[256,128]{1,0:T(8,128)S(1)}, f32[256,128]{1,0:T(8,128)S(1)}, f32[256,128]{1,0:T(8,128)S(1)}, f32[256,512]{1,0:T(8,128)S(1)}) custom-call(bf16[16,256]{1,0:T(8,128)(2,1)S(1)} %concatenate.3.k_ref, bf16[272,128]{1,0:T(8,128)(2,1)S(1)} %copy-done.1, ...), custom_call_target="tpu_custom_call" | custom-call | flops 2000000000 | bytes 2000000 | tf_op jit(solution)/shard_map/pallas_call | solution.py:154
  10.1 0.4 collective-permute-done.1.refs_0_.below_ref.refs_9_
  10.5 0.8 %collective-permute-done.2.refs_1_.above_ref.refs_11_ = bf16[272,128]{1,0:T(8,128)(2,1)S(1)} collective-permute-done((bf16[272,128]{1,0:T(8,128)(2,1)}, bf16[272,128]{1,0:T(8,128)(2,1)S(1)}, u32[]{:S(2)}, u32[]{:S(2)}) %collective-permute-start.2) | collective-permute-done | bytes 69664 | tf_op jit(solution)/shard_map/ppermute | solution.py:516
  11.4 0.5 %collective-permute-start.4 = (bf16[272,128]{1,0:T(8,128)(2,1)S(1)}, bf16[272,128]{1,0:T(8,128)(2,1)S(1)}, u32[]{:S(2)}, u32[]{:S(2)}) collective-permute-start(bf16[272,128]{1,0:T(8,128)(2,1)S(1)} %collective-permute-done.2.refs_1_.above_ref.refs_11_), channel_id=1, source_target_pairs={{0,4},{4,0},{8,12},{12,8},{16,20},{20,16},{24,28},{28,24},{1,5},{5... | collective-permute-start | bytes 208904 | tf_op jit(solution)/shard_map/ppermute | solution.py:521
  11.9 2.1 %collective-permute-start.7 = (bf16[48,128]{1,0:T(8,128)(2,1)S(1)}, bf16[48,128]{1,0:T(8,128)(2,1)S(1)}, u32[]{:S(2)}, u32[]{:S(2)}) collective-permute-start(bf16[48,128]{1,0:T(8,128)(2,1)S(1)} %copy-done.7), channel_id=1, source_target_pairs={{0,28},{4,8},{8,4},{12,16},{16,12},{20,24},{24,20},{28,0},{1,29},{... | collective-permute-start | bytes 36872 | tf_op jit(solution)/shard_map/ppermute | solution.py:554
  13.9 1.0 %collective-permute-done.5.refs_0_.refs_10_ = bf16[272,128]{1,0:T(8,128)(2,1)S(1)} collective-permute-done((bf16[272,128]{1,0:T(8,128)(2,1)}, bf16[272,128]{1,0:T(8,128)(2,1)S(1)}, u32[]{:S(2)}, u32[]{:S(2)}) %collective-permute-start.5) | collective-permute-done | bytes 69664 | tf_op jit(solution)/shard_map/ppermute | solution.py:516
  14.9 0.9 %shard_map.129 = (f32[256,128]{1,0:T(8,128)S(1)}, f32[256,128]{1,0:T(8,128)S(1)}, f32[256,128]{1,0:T(8,128)S(1)}, f32[256,128]{1,0:T(8,128)S(1)}, f32[256,128]{1...) custom-call(bf16[16,256]{1,0:T(8,128)(2,1)S(1)} %concatenate.3.k_ref, ...), custom_call_target="tpu_custom_call" | custom-call | flops 4000000000 | bytes 4000000 | tf_op jit(solution)/shard_map/pallas_call | solution.py:154
  16.2 0.6 %shard_map.130 = (f32[256,128]{1,0:T(8,128)S(1)}, f32[256,128]{1,0:T(8,128)S(1)}, f32[256,128]{1,0:T(8,128)S(1)}, f32[256,128]{1,0:T(8,128)S(1)}, f32[64,512]{1,...) custom-call(bf16[16,256]{1,0:T(8,128)(2,1)S(1)} %concatenate.3.k_ref, ...), custom_call_target="tpu_custom_call" | custom-call | flops 2000000000 | bytes 2000000 | tf_op jit(solution)/shard_map/pallas_call | solution.py:154
  16.8 1.6 %collective-permute-start.8 = (bf16[64,512]{1,0:T(8,128)(2,1)S(1)}, bf16[64,512]{1,0:T(8,128)(2,1)S(1)}, u32[]{:S(2)}, u32[]{:S(2)}) collective-permute-start(bf16[64,512]{1,0:T(8,128)(2,1)S(1)} %get-tuple-element.69), channel_id=1, source_target_pairs={{0,8},{4,12},{8,0},{12,4},{16,24},{20,28},{24,16},{28,20},{1,9},{5... | collective-permute-start | bytes 196616 | tf_op jit(solution)/shard_map/ppermute | solution.py:521
  18.4 1.5 %collective-permute-start.9 = (bf16[64,512]{1,0:T(8,128)(2,1)S(1)}, bf16[64,512]{1,0:T(8,128)(2,1)S(1)}, u32[]{:S(2)}, u32[]{:S(2)}) collective-permute-start(bf16[64,512]{1,0:T(8,128)(2,1)S(1)} %get-tuple-element.70), channel_id=1, source_target_pairs={{0,16},{4,20},{8,24},{12,28},{16,0},{20,4},{24,8},{28,12},{1,17},{... | collective-permute-start | bytes 196616 | tf_op jit(solution)/shard_map/ppermute | solution.py:521
  19.9 0.5 %collective-permute-start.10 = (bf16[64,512]{1,0:T(8,128)(2,1)S(1)}, bf16[64,512]{1,0:T(8,128)(2,1)S(1)}, u32[]{:S(2)}, u32[]{:S(2)}) collective-permute-start(bf16[64,512]{1,0:T(8,128)(2,1)S(1)} %get-tuple-element.71), channel_id=1, source_target_pairs={{0,24},{4,28},{8,16},{12,20},{16,8},{20,12},{24,0},{28,4},{1,25},{... | collective-permute-start | bytes 196616 | tf_op jit(solution)/shard_map/ppermute | solution.py:521
  20.5 2.3 %pairs.1 = (f32[192,128]{1,0:T(8,128)S(1)}, f32[8,256]{1,0:T(8,128)S(1)}, f32[144,128]{1,0:T(8,128)S(1)}, bf16[48,512]{1,0:T(8,128)(2,1)S(1)}) custom-call(f32[8,128]{1,0:T(8,128)S(1)} %iota.10.where_ref, bf16[272,128]{1,0:T(8,128)(2,1)S(1)} %copy-done.1, bf16[272,128]{1,0:T(8,128)(2,1)S(1)} %collective-permute-done.refs_1_.flip_ref.refs_8_, ...), custom_call_target="tpu_custom_call" | custom-call | flops 4000000000 | bytes 1000000 | tf_op jit(solution)/shard_map/pairs/pallas_call | solution.py:461
  22.8 2.2 %collective-permute-done.10.refs_2_ = bf16[64,512]{1,0:T(8,128)(2,1)S(1)} collective-permute-done((bf16[64,512]{1,0:T(8,128)(2,1)S(1)}, bf16[64,512]{1,0:T(8,128)(2,1)S(1)}, u32[]{:S(2)}, u32[]{:S(2)}) %collective-permute-start.10) | collective-permute-done | bytes 65568 | tf_op jit(solution)/shard_map/ppermute | solution.py:521
  25.1 0.6 %collective-permute-start.11 = (bf16[112,512]{1,0:T(8,128)(2,1)S(1)}, bf16[112,512]{1,0:T(8,128)(2,1)S(1)}, u32[]{:S(2)}, u32[]{:S(2)}) collective-permute-start(bf16[112,512]{1,0:T(8,128)(2,1)S(1)} %get-tuple-element.74.refs_12_), channel_id=1, source_target_pairs={{0,8},{4,12},{8,0},{12,4},{16,24},{20,28},{24,16},{28,20},{1,9},{5... | collective-permute-start | bytes 344072 | tf_op jit(solution)/shard_map/ppermute | solution.py:521
  25.7 0.5 %collective-permute-start.12 = (bf16[112,512]{1,0:T(8,128)(2,1)S(1)}, bf16[112,512]{1,0:T(8,128)(2,1)S(1)}, u32[]{:S(2)}, u32[]{:S(2)}) collective-permute-start(bf16[112,512]{1,0:T(8,128)(2,1)S(1)} %get-tuple-element.74.refs_12_), channel_id=1, source_target_pairs={{0,16},{4,20},{8,24},{12,28},{16,0},{20,4},{24,8},{28,12},{1,17},{... | collective-permute-start | bytes 344072 | tf_op jit(solution)/shard_map/ppermute | solution.py:521
  26.2 2.4 %collective-permute-start.13 = (bf16[112,512]{1,0:T(8,128)(2,1)S(1)}, bf16[112,512]{1,0:T(8,128)(2,1)S(1)}, u32[]{:S(2)}, u32[]{:S(2)}) collective-permute-start(bf16[112,512]{1,0:T(8,128)(2,1)S(1)} %get-tuple-element.74.refs_12_), channel_id=1, source_target_pairs={{0,24},{4,28},{8,16},{12,20},{16,8},{20,12},{24,0},{28,4},{1,25},{... | collective-permute-start | bytes 344072 | tf_op jit(solution)/shard_map/ppermute | solution.py:521
  28.7 1.5 %collective-permute-done.11.refs_13_ = bf16[112,512]{1,0:T(8,128)(2,1)S(1)} collective-permute-done((bf16[112,512]{1,0:T(8,128)(2,1)S(1)}, bf16[112,512]{1,0:T(8,128)(2,1)S(1)}, u32[]{:S(2)}, u32[]{:S(2)}) %collective-permute-start.11) | collective-permute-done | bytes 114720 | tf_op jit(solution)/shard_map/ppermute | solution.py:521
  30.2 1.9 %collective-permute-done.12.refs_14_ = bf16[112,512]{1,0:T(8,128)(2,1)S(1)} collective-permute-done((bf16[112,512]{1,0:T(8,128)(2,1)S(1)}, bf16[112,512]{1,0:T(8,128)(2,1)S(1)}, u32[]{:S(2)}, u32[]{:S(2)}) %collective-permute-start.12) | collective-permute-done | bytes 114720 | tf_op jit(solution)/shard_map/ppermute | solution.py:521
  32.1 0.7 %shard_map.132.there_ref = f32[688,128]{1,0:T(8,128)S(1)} custom-call(f32[8,128]{1,0:T(8,128)S(1)} %iota.10.where_ref, bf16[16,256]{1,0:T(8,128)(2,1)S(1)} %concatenate.3.k_ref, f32[256,128]{1,0:T(8,128)S(1)} %get-tuple-element.77.refs_0_, f32[256,128]{1,0:T(8,128)S(1)} %get-tuple-element.78.refs_1_, f32[256,128]{1,0:T(8,128)S(1)} %get-tuple-element.79.refs_2_, ...), custom_call_target="tpu_custom_call" | custom-call | flops 3000000000 | bytes 4000000 | tf_op jit(solution)/shard_map/pallas_call | solution.py:328
  32.8 0.7 %shard_map.131.here_ref = f32[544,128]{1,0:T(8,128)S(1)} custom-call(bf16[16,256]{1,0:T(8,128)(2,1)S(1)} %concatenate.3.k_ref, f32[256,128]{1,0:T(8,128)S(1)} %get-tuple-element.51.refs_0_, f32[256,128]{1,0:T(8,128)S(1)} %get-tuple-element.57.refs_1_, f32[256,128]{1,0:T(8,128)S(1)} %get-tuple-element.59.refs_2_, f32[256,128]{1,0:T(8,128)S(1)} %get-tuple-element.60.refs_3_, ...), custom_call_target="tpu_custom_call" | custom-call | flops 3000000000 | bytes 4000000 | tf_op jit(solution)/shard_map/pallas_call | solution.py:328
  33.5 1.0 %collective-permute-done.14.sent_ref = f32[688,128]{1,0:T(8,128)S(1)} collective-permute-done((f32[688,128]{1,0:T(8,128)S(1)}, f32[688,128]{1,0:T(8,128)S(1)}, u32[]{:S(2)}, u32[]{:S(2)}) %collective-permute-start.14) | collective-permute-done | bytes 352288 | tf_op jit(solution)/shard_map/ppermute | solution.py:521
  34.5 0.8 %collective-permute-start.15 = (bf16[288,128]{1,0:T(8,128)(2,1)S(1)}, bf16[288,128]{1,0:T(8,128)(2,1)S(1)}, u32[]{:S(2)}, u32[]{:S(2)}) collective-permute-start(bf16[288,128]{1,0:T(8,128)(2,1)S(1)} %get-tuple-element.88), channel_id=1, source_target_pairs={{2,0},{3,1},{0,2},{1,3},{6,4},{7,5},{4,6},{5,7},{10,8},{11,9},{8,1... | collective-permute-start | bytes 221192 | tf_op jit(solution)/shard_map/ppermute | solution.py:516
  35.3 3.2 %collective-permute-start.16 = (bf16[288,128]{1,0:T(8,128)(2,1)S(1)}, bf16[288,128]{1,0:T(8,128)(2,1)S(1)}, u32[]{:S(2)}, u32[]{:S(2)}) collective-permute-start(bf16[288,128]{1,0:T(8,128)(2,1)S(1)} %get-tuple-element.89), channel_id=1, source_target_pairs={{1,0},{2,1},{3,2},{0,3},{5,4},{6,5},{7,6},{4,7},{9,8},{10,9},{11,1... | collective-permute-start | bytes 221192 | tf_op jit(solution)/shard_map/ppermute | solution.py:516
  38.5 3.5 %collective-permute-done.15.refs_0_ = bf16[288,128]{1,0:T(8,128)(2,1)S(1)} collective-permute-done((bf16[288,128]{1,0:T(8,128)(2,1)S(1)}, bf16[288,128]{1,0:T(8,128)(2,1)S(1)}, u32[]{:S(2)}, u32[]{:S(2)}) %collective-permute-start.15) | collective-permute-done | bytes 73760 | tf_op jit(solution)/shard_map/ppermute | solution.py:516
  42.0 2.6 %collective-permute-done.17.refs_2_ = bf16[288,128]{1,0:T(8,128)(2,1)S(1)} collective-permute-done((bf16[288,128]{1,0:T(8,128)(2,1)S(1)}, bf16[288,128]{1,0:T(8,128)(2,1)S(1)}, u32[]{:S(2)}, u32[]{:S(2)}) %collective-permute-start.17) | collective-permute-done | bytes 73760 | tf_op jit(solution)/shard_map/ppermute | solution.py:516
  44.6 0.7 %finish.1 = (f32[128,128]{1,0:T(8,128)}, f32[3,128]{1,0:T(4,128)}, f32[64,128]{1,0:T(8,128)}, f32[16,128]{1,0:T(8,128)}, f32[128,128]{1,0:T(8,128)}) custom-call(f32[280,128]{1,0:T(8,128)S(1)} %get-tuple-element.86.own_ref, f32[64,512]{1,0:T(8,128)S(1)} %get-tuple-element.87.total_ref, bf16[288,128]{1,0:T(8,128)(2,1)S(1)} %collective-permute-done.15.refs_0_, ...), custom_call_target="tpu_custom_call" | custom-call | tf_op jit(solution)/shard_map/finish/pallas_call | solution.py:500
  (42 shorter events, 1.1 us)
Async XLA Ops:
  0.6 8.1 %copy-start = (f32[2048,128]{1,0:T(8,128)S(1)}, f32[2048,128]{1,0:T(8,128)}, u32[]{:S(2)}) copy-start(f32[2048,128]{1,0:T(8,128)} %param.15) | copy-start | bytes 3145732
  2.2 6.2 %copy-start.6 = (s32[3,2048]{1,0:T(4,128)S(1)}, s32[3,2048]{1,0:T(4,128)}, u32[]{:S(2)}) copy-start(s32[3,2048]{1,0:T(4,128)} %param.14) | copy-start | bytes 73732
  2.2 6.7 %collective-permute-start = (bf16[272,128]{1,0:T(8,128)(2,1)}, bf16[272,128]{1,0:T(8,128)(2,1)S(1)}, u32[]{:S(2)}, u32[]{:S(2)}) collective-permute-start(bf16[272,128]{1,0:T(8,128)(2,1)} %get-tuple-element.50.refs_0_.own_ref.refs_8_), channel_id=1, source_target_pairs={{0,4},{4,0},{8,12},{12,8},{16,20},{20,16},{24,28},{28,24},{1,5},{5... | collective-permute-start | bytes 208904 | tf_op jit(solution)/shard_map/ppermute | solution.py:521
  2.8 7.8 %collective-permute-start.1 = (bf16[272,128]{1,0:T(8,128)(2,1)}, bf16[272,128]{1,0:T(8,128)(2,1)S(1)}, u32[]{:S(2)}, u32[]{:S(2)}) collective-permute-start(bf16[272,128]{1,0:T(8,128)(2,1)} %get-tuple-element.50.refs_0_.own_ref.refs_8_), channel_id=1, source_target_pairs={{3,0},{0,1},{1,2},{2,3},{7,4},{4,5},{5,6},{6,7},{11,8},{8,9},{9,10... | collective-permute-start | bytes 208904 | tf_op jit(solution)/shard_map/ppermute | solution.py:516
  5.4 6.0 %collective-permute-start.2 = (bf16[272,128]{1,0:T(8,128)(2,1)}, bf16[272,128]{1,0:T(8,128)(2,1)S(1)}, u32[]{:S(2)}, u32[]{:S(2)}) collective-permute-start(bf16[272,128]{1,0:T(8,128)(2,1)} %get-tuple-element.50.refs_0_.own_ref.refs_8_), channel_id=1, source_target_pairs={{1,0},{2,1},{3,2},{0,3},{5,4},{6,5},{7,6},{4,7},{9,8},{10,9},{11,1... | collective-permute-start | bytes 208904 | tf_op jit(solution)/shard_map/ppermute | solution.py:516
  7.5 7.4 %collective-permute-start.5 = (bf16[272,128]{1,0:T(8,128)(2,1)}, bf16[272,128]{1,0:T(8,128)(2,1)S(1)}, u32[]{:S(2)}, u32[]{:S(2)}) collective-permute-start(bf16[272,128]{1,0:T(8,128)(2,1)} %get-tuple-element.50.refs_0_.own_ref.refs_8_), channel_id=1, source_target_pairs={{2,0},{3,1},{0,2},{1,3},{6,4},{7,5},{4,6},{5,7},{10,8},{11,9},{8,1... | collective-permute-start | bytes 208904 | tf_op jit(solution)/shard_map/ppermute | solution.py:516
  8.6 0.9 %copy-start.1 = (bf16[272,128]{1,0:T(8,128)(2,1)S(1)}, bf16[272,128]{1,0:T(8,128)(2,1)}, u32[]{:S(2)}) copy-start(bf16[272,128]{1,0:T(8,128)(2,1)} %get-tuple-element.50.refs_0_.own_ref.refs_8_) | copy-start | bytes 208900
  8.9 3.0 %copy-start.7 = (bf16[48,128]{1,0:T(8,128)(2,1)S(1)}, bf16[48,128]{1,0:T(8,128)(2,1)}, u32[]{:S(2)}) copy-start(bf16[48,128]{1,0:T(8,128)(2,1)} %get-tuple-element.68) | copy-start | bytes 36868
  11.3 3.6 %collective-permute-start.3 = (bf16[272,128]{1,0:T(8,128)(2,1)S(1)}, bf16[272,128]{1,0:T(8,128)(2,1)S(1)}, u32[]{:S(2)}, u32[]{:S(2)}) collective-permute-start(bf16[272,128]{1,0:T(8,128)(2,1)S(1)} %collective-permute-done.1.refs_0_.below_ref.refs_9_), channel_id=1, source_target_pairs={{0,4},{4,0},{8,12},{12,8},{16,20},{20,16},{24,28},{28,24},{1,5},{5... | collective-permute-start | bytes 208904 | tf_op jit(solution)/shard_map/ppermute | solution.py:521
  11.4 3.6 %collective-permute-start.4 = (bf16[272,128]{1,0:T(8,128)(2,1)S(1)}, bf16[272,128]{1,0:T(8,128)(2,1)S(1)}, u32[]{:S(2)}, u32[]{:S(2)}) collective-permute-start(bf16[272,128]{1,0:T(8,128)(2,1)S(1)} %collective-permute-done.2.refs_1_.above_ref.refs_11_), channel_id=1, source_target_pairs={{0,4},{4,0},{8,12},{12,8},{16,20},{20,16},{24,28},{28,24},{1,5},{5... | collective-permute-start | bytes 208904 | tf_op jit(solution)/shard_map/ppermute | solution.py:521
  11.9 8.5 %collective-permute-start.7 = (bf16[48,128]{1,0:T(8,128)(2,1)S(1)}, bf16[48,128]{1,0:T(8,128)(2,1)S(1)}, u32[]{:S(2)}, u32[]{:S(2)}) collective-permute-start(bf16[48,128]{1,0:T(8,128)(2,1)S(1)} %copy-done.7), channel_id=1, source_target_pairs={{0,28},{4,8},{8,4},{12,16},{16,12},{20,24},{24,20},{28,0},{1,29},{... | collective-permute-start | bytes 36872 | tf_op jit(solution)/shard_map/ppermute | solution.py:554
  14.9 1.3 %collective-permute-start.6 = (bf16[272,128]{1,0:T(8,128)(2,1)S(1)}, bf16[272,128]{1,0:T(8,128)(2,1)S(1)}, u32[]{:S(2)}, u32[]{:S(2)}) collective-permute-start(bf16[272,128]{1,0:T(8,128)(2,1)S(1)} %collective-permute-done.5.refs_0_.refs_10_), channel_id=1, source_target_pairs={{0,4},{4,0},{8,12},{12,8},{16,20},{20,16},{24,28},{28,24},{1,5},{5... | collective-permute-start | bytes 208904 | tf_op jit(solution)/shard_map/ppermute | solution.py:521
  16.2 4.2 %copy-start.2 = (bf16[128,128]{1,0:T(8,128)(2,1)S(1)}, bf16[128,128]{1,0:T(8,128)(2,1)}, u32[]{:S(2)}) copy-start(bf16[128,128]{1,0:T(8,128)(2,1)} %wo_ref.1) | copy-start | bytes 98308
  16.2 4.2 %copy-start.3 = (s32[16,128]{1,0:T(8,128)S(1)}, s32[16,128]{1,0:T(8,128)}, u32[]{:S(2)}) copy-start(s32[16,128]{1,0:T(8,128)} %nbr_ref.1) | copy-start | bytes 24580
  16.8 3.6 %copy-start.4 = (bf16[16,128]{1,0:T(8,128)(2,1)S(1)}, bf16[16,128]{1,0:T(8,128)(2,1)}, u32[]{:S(2)}) copy-start(bf16[16,128]{1,0:T(8,128)(2,1)} %wr_ref.1) | copy-start | bytes 12292
  16.8 6.0 %collective-permute-start.8 = (bf16[64,512]{1,0:T(8,128)(2,1)S(1)}, bf16[64,512]{1,0:T(8,128)(2,1)S(1)}, u32[]{:S(2)}, u32[]{:S(2)}) collective-permute-start(bf16[64,512]{1,0:T(8,128)(2,1)S(1)} %get-tuple-element.69), channel_id=1, source_target_pairs={{0,8},{4,12},{8,0},{12,4},{16,24},{20,28},{24,16},{28,20},{1,9},{5... | collective-permute-start | bytes 196616 | tf_op jit(solution)/shard_map/ppermute | solution.py:521
  18.4 4.4 %collective-permute-start.9 = (bf16[64,512]{1,0:T(8,128)(2,1)S(1)}, bf16[64,512]{1,0:T(8,128)(2,1)S(1)}, u32[]{:S(2)}, u32[]{:S(2)}) collective-permute-start(bf16[64,512]{1,0:T(8,128)(2,1)S(1)} %get-tuple-element.70), channel_id=1, source_target_pairs={{0,16},{4,20},{8,24},{12,28},{16,0},{20,4},{24,8},{28,12},{1,17},{... | collective-permute-start | bytes 196616 | tf_op jit(solution)/shard_map/ppermute | solution.py:521
  19.9 0.7 %copy-start.5 = (s32[128]{0:T(128)S(1)}, s32[128]{0:T(128)}, u32[]{:S(2)}) copy-start(s32[128]{0:T(128)} %param.13) | copy-start | bytes 1540
  19.9 5.2 %collective-permute-start.10 = (bf16[64,512]{1,0:T(8,128)(2,1)S(1)}, bf16[64,512]{1,0:T(8,128)(2,1)S(1)}, u32[]{:S(2)}, u32[]{:S(2)}) collective-permute-start(bf16[64,512]{1,0:T(8,128)(2,1)S(1)} %get-tuple-element.71), channel_id=1, source_target_pairs={{0,24},{4,28},{8,16},{12,20},{16,8},{20,12},{24,0},{28,4},{1,25},{... | collective-permute-start | bytes 196616 | tf_op jit(solution)/shard_map/ppermute | solution.py:521
  25.1 5.1 %collective-permute-start.11 = (bf16[112,512]{1,0:T(8,128)(2,1)S(1)}, bf16[112,512]{1,0:T(8,128)(2,1)S(1)}, u32[]{:S(2)}, u32[]{:S(2)}) collective-permute-start(bf16[112,512]{1,0:T(8,128)(2,1)S(1)} %get-tuple-element.74.refs_12_), channel_id=1, source_target_pairs={{0,8},{4,12},{8,0},{12,4},{16,24},{20,28},{24,16},{28,20},{1,9},{5... | collective-permute-start | bytes 344072 | tf_op jit(solution)/shard_map/ppermute | solution.py:521
  25.7 6.4 %collective-permute-start.12 = (bf16[112,512]{1,0:T(8,128)(2,1)S(1)}, bf16[112,512]{1,0:T(8,128)(2,1)S(1)}, u32[]{:S(2)}, u32[]{:S(2)}) collective-permute-start(bf16[112,512]{1,0:T(8,128)(2,1)S(1)} %get-tuple-element.74.refs_12_), channel_id=1, source_target_pairs={{0,16},{4,20},{8,24},{12,28},{16,0},{20,4},{24,8},{28,12},{1,17},{... | collective-permute-start | bytes 344072 | tf_op jit(solution)/shard_map/ppermute | solution.py:521
  26.2 5.9 %collective-permute-start.13 = (bf16[112,512]{1,0:T(8,128)(2,1)S(1)}, bf16[112,512]{1,0:T(8,128)(2,1)S(1)}, u32[]{:S(2)}, u32[]{:S(2)}) collective-permute-start(bf16[112,512]{1,0:T(8,128)(2,1)S(1)} %get-tuple-element.74.refs_12_), channel_id=1, source_target_pairs={{0,24},{4,28},{8,16},{12,20},{16,8},{20,12},{24,0},{28,4},{1,25},{... | collective-permute-start | bytes 344072 | tf_op jit(solution)/shard_map/ppermute | solution.py:521
  32.8 1.7 %collective-permute-start.14 = (f32[688,128]{1,0:T(8,128)S(1)}, f32[688,128]{1,0:T(8,128)S(1)}, u32[]{:S(2)}, u32[]{:S(2)}) collective-permute-start(f32[688,128]{1,0:T(8,128)S(1)} %shard_map.132.there_ref), channel_id=1, source_target_pairs={{0,4},{4,0},{8,12},{12,8},{16,20},{20,16},{24,28},{28,24},{1,5},{5... | collective-permute-start | bytes 1056776 | tf_op jit(solution)/shard_map/ppermute | solution.py:521
  34.5 7.5 %collective-permute-start.15 = (bf16[288,128]{1,0:T(8,128)(2,1)S(1)}, bf16[288,128]{1,0:T(8,128)(2,1)S(1)}, u32[]{:S(2)}, u32[]{:S(2)}) collective-permute-start(bf16[288,128]{1,0:T(8,128)(2,1)S(1)} %get-tuple-element.88), channel_id=1, source_target_pairs={{2,0},{3,1},{0,2},{1,3},{6,4},{7,5},{4,6},{5,7},{10,8},{11,9},{8,1... | collective-permute-start | bytes 221192 | tf_op jit(solution)/shard_map/ppermute | solution.py:516
  35.3 6.7 %collective-permute-start.16 = (bf16[288,128]{1,0:T(8,128)(2,1)S(1)}, bf16[288,128]{1,0:T(8,128)(2,1)S(1)}, u32[]{:S(2)}, u32[]{:S(2)}) collective-permute-start(bf16[288,128]{1,0:T(8,128)(2,1)S(1)} %get-tuple-element.89), channel_id=1, source_target_pairs={{1,0},{2,1},{3,2},{0,3},{5,4},{6,5},{7,6},{4,7},{9,8},{10,9},{11,1... | collective-permute-start | bytes 221192 | tf_op jit(solution)/shard_map/ppermute | solution.py:516
  38.4 6.2 %collective-permute-start.17 = (bf16[288,128]{1,0:T(8,128)(2,1)S(1)}, bf16[288,128]{1,0:T(8,128)(2,1)S(1)}, u32[]{:S(2)}, u32[]{:S(2)}) collective-permute-start(bf16[288,128]{1,0:T(8,128)(2,1)S(1)} %get-tuple-element.90), channel_id=1, source_target_pairs={{3,0},{0,1},{1,2},{2,3},{7,4},{4,5},{5,6},{6,7},{11,8},{8,9},{9,10... | collective-permute-start | bytes 221192 | tf_op jit(solution)/shard_map/ppermute | solution.py:516
where the time goes:
time: 45.5 us; the launch traced here: 45.3 us
  starting transfers between devices  19.9 us (44%)
  waiting for transfers between devices  15.3 us (34%)
  Pallas kernels  8.12 us (18%)
  local copies, waits for them, and re-layouts  1.15 us (3%)
  between operations  0.78 us (2%)
    ppermute x6, starting transfers between devices, along(): return lax.ppermute(block, axis, [((i - shift) % n, i) for i in range(n)])  9.62 us
    ppermute x6, waiting for transfers between devices, along(): return lax.ppermute(block, axis, [((i - shift) % n, i) for i in range(n)])  8.36 us
    ppermute x11, starting transfers between devices, swapped(): return lax.ppermute(block, axis, [(i, i ^ mask) for i in range(n)])  8.22 us
    ppermute x11, waiting for transfers between devices, swapped(): return lax.ppermute(block, axis, [(i, i ^ mask) for i in range(n)])  6.97 us
    pallas_call x1, Pallas kernels, pair_part(): pl.pallas_call(functools.partial(pair_body, atoms, channels, group, pos_u...  2.25 us
    pallas_call x3, Pallas kernels, structure(): pl.pallas_call(functools.partial(structure_body, atoms, n, partial is not...  2.16 us
    ppermute x1, starting transfers between devices, program(): cross = lax.ppermute(faces, 'dom', across)  2.05 us
    pallas_call x1, Pallas kernels, pack(): pl.pallas_call(pack_body, out_shape=(jax.ShapeDtypeStruct((2 * atoms + PO...  1.54 us
  transfers between devices with their start and end apart: 18, of which 10 were waited for; matrix products, arithmetic and copies ran while one was open for 1% of the time, Pallas kernels for 11%

commit v1 on v0

--- a/solution.py
+++ b/solution.py
@@ -320,8 +320,8 @@
         out = out_refs[d - 1]
         out[:atoms, :] = rows.astype(BF16)
         spots = jnp.where(row < 3, spots, 0.0)
-        out[atoms : atoms + POS_ROWS, :] = jnp.concatenate(packed(spots), axis=0)
-        out[atoms + POS_ROWS :, :] = grad
+        out[atoms : atoms + grad.shape[0], :] = grad
+        out[atoms + grad.shape[0] :, :] = packed(spots)[0]
 
 
 def back_call(body, out_shape, *operands):
@@ -483,8 +483,8 @@
     feat, place, grad = own_ref[:atoms], own_ref[atoms : atoms + 8], own_ref[atoms + 8 :]
     for m in msgs:
         feat = feat + m[:atoms].astype(F32)
-        place = place + pos_of(m[atoms : atoms + POS_ROWS])
-        grad = grad + m[atoms + POS_ROWS :].astype(F32)
+        place = place + pos_of(m[atoms + grad.shape[0] :], 2)
+        grad = grad + m[atoms : atoms + grad.shape[0]].astype(F32)
     levels = radial_ref.shape[0]
     c = feat_ref.shape[1]
     re = total_ref[:, :c] * total_ref[:, c : 2 * c]
@@ -630,7 +630,7 @@
         buf,
         moves,
     )
-    message = jax.ShapeDtypeStruct((atoms + POS_ROWS + grads.shape[0], channels), BF16)
+    message = jax.ShapeDtypeStruct((atoms + grads.shape[0] + 8, channels), BF16)
     own_sum, *partials = back_call(
         functools.partial(join_body, atoms, n_slab),
         (jax.ShapeDtypeStruct((atoms + 8 + grads.shape[0], channels), F32),)

time: 45.5 us -> 45.5 us (level)
  no operation moved by 1% of the time
where the time goes in v1:
time: 45.5 us; the launch traced here: 45.3 us
  starting transfers between devices  19.9 us (44%)
  waiting for transfers between devices  15.3 us (34%)
  Pallas kernels  8.11 us (18%)
  local copies, waits for them, and re-layouts  1.15 us (3%)
  between operations  0.78 us (2%)
    ppermute x6, starting transfers between devices, along(): return lax.ppermute(block, axis, [((i - shift) % n, i) for i in range(n)])  9.62 us
    ppermute x6, waiting for transfers between devices, along(): return lax.ppermute(block, axis, [((i - shift) % n, i) for i in range(n)])  8.33 us
    ppermute x11, starting transfers between devices, swapped(): return lax.ppermute(block, axis, [(i, i ^ mask) for i in range(n)])  8.22 us
    ppermute x11, waiting for transfers between devices, swapped(): return lax.ppermute(block, axis, [(i, i ^ mask) for i in range(n)])  6.97 us
    pallas_call x1, Pallas kernels, pair_part(): pl.pallas_call(functools.partial(pair_body, atoms, channels, group, pos_u...  2.25 us
    pallas_call x3, Pallas kernels, structure(): pl.pallas_call(functools.partial(structure_body, atoms, n, partial is not...  2.16 us
    ppermute x1, starting transfers between devices, program(): cross = lax.ppermute(faces, 'dom', across)  2.05 us
    pallas_call x1, Pallas kernels, pack(): pl.pallas_call(pack_body, out_shape=(jax.ShapeDtypeStruct((2 * atoms + PO...  1.54 us
  transfers between devices with their start and end apart: 18, of which 10 were waited for; matrix products, arithmetic and copies ran while one was open for 1% of the time, Pallas kernels for 11%

profile of v1, /device:TPU:0, one launch (start us, length us, event | category | flops | bytes accessed | tf_op | source)
XLA Modules:
  0.0 45.3 jit_solution(4926920392647241128)
XLA Ops:
  0.6 1.5 %pack.1 = (bf16[272,128]{1,0:T(8,128)(2,1)}, bf16[48,128]{1,0:T(8,128)(2,1)}) custom-call(bf16[128,128]{1,0:T(8,128)(2,1)} %feat_hbm.1, bf16[128,128]{1,0:T(8,128)(2,1)} %cot_hbm.1, f32[3,128]{1,0:T(4,128)} %pos_hbm.1), custom_call_target="tpu_custom_call" | custom-call | tf_op jit(solution)/shard_map/pack/pallas_call | solution.py:103
  2.2 0.6 %collective-permute-start = (bf16[272,128]{1,0:T(8,128)(2,1)}, bf16[272,128]{1,0:T(8,128)(2,1)S(1)}, u32[]{:S(2)}, u32[]{:S(2)}) collective-permute-start(bf16[272,128]{1,0:T(8,128)(2,1)} %get-tuple-element.50.refs_0_.own_ref.refs_8_), channel_id=1, source_target_pairs={{0,4},{4,0},{8,12},{12,8},{16,20},{20,16},{24,28},{28,24},{1,5},{5... | collective-permute-start | bytes 208904 | tf_op jit(solution)/shard_map/ppermute | solution.py:521
  2.8 2.6 %collective-permute-start.1 = (bf16[272,128]{1,0:T(8,128)(2,1)}, bf16[272,128]{1,0:T(8,128)(2,1)S(1)}, u32[]{:S(2)}, u32[]{:S(2)}) collective-permute-start(bf16[272,128]{1,0:T(8,128)(2,1)} %get-tuple-element.50.refs_0_.own_ref.refs_8_), channel_id=1, source_target_pairs={{3,0},{0,1},{1,2},{2,3},{7,4},{4,5},{5,6},{6,7},{11,8},{8,9},{9,10... | collective-permute-start | bytes 208904 | tf_op jit(solution)/shard_map/ppermute | solution.py:516
  5.4 2.1 %collective-permute-start.2 = (bf16[272,128]{1,0:T(8,128)(2,1)}, bf16[272,128]{1,0:T(8,128)(2,1)S(1)}, u32[]{:S(2)}, u32[]{:S(2)}) collective-permute-start(bf16[272,128]{1,0:T(8,128)(2,1)} %get-tuple-element.50.refs_0_.own_ref.refs_8_), channel_id=1, source_target_pairs={{1,0},{2,1},{3,2},{0,3},{5,4},{6,5},{7,6},{4,7},{9,8},{10,9},{11,1... | collective-permute-start | bytes 208904 | tf_op jit(solution)/shard_map/ppermute | solution.py:516
  7.5 0.9 %collective-permute-start.5 = (bf16[272,128]{1,0:T(8,128)(2,1)}, bf16[272,128]{1,0:T(8,128)(2,1)S(1)}, u32[]{:S(2)}, u32[]{:S(2)}) collective-permute-start(bf16[272,128]{1,0:T(8,128)(2,1)} %get-tuple-element.50.refs_0_.own_ref.refs_8_), channel_id=1, source_target_pairs={{2,0},{3,1},{0,2},{1,3},{6,4},{7,5},{4,6},{5,7},{10,8},{11,9},{8,1... | collective-permute-start | bytes 208904 | tf_op jit(solution)/shard_map/ppermute | solution.py:516
  8.9 0.6 %copy-done.1 = bf16[272,128]{1,0:T(8,128)(2,1)S(1)} copy-done((bf16[272,128]{1,0:T(8,128)(2,1)S(1)}, bf16[272,128]{1,0:T(8,128)(2,1)}, u32[]{:S(2)}) %copy-start.1) | copy-done | bytes 69656
  9.5 0.6 %shard_map.128 = (f32[256,128]{1,0:T(8,128)S(1)}, f32[256,128]{1,0:T(8,128)S(1)}, f32[256,128]{1,0:T(8,128)S(1)}, f32[256,128]{1,0:T(8,128)S(1)}, f32[256,512]{1,0:T(8,128)S(1)}) custom-call(bf16[16,256]{1,0:T(8,128)(2,1)S(1)} %concatenate.3.k_ref, bf16[272,128]{1,0:T(8,128)(2,1)S(1)} %copy-done.1, ...), custom_call_target="tpu_custom_call" | custom-call | flops 2000000000 | bytes 2000000 | tf_op jit(solution)/shard_map/pallas_call | solution.py:154
  10.1 0.4 collective-permute-done.1.refs_0_.below_ref.refs_9_
  10.5 0.8 %collective-permute-done.2.refs_1_.above_ref.refs_11_ = bf16[272,128]{1,0:T(8,128)(2,1)S(1)} collective-permute-done((bf16[272,128]{1,0:T(8,128)(2,1)}, bf16[272,128]{1,0:T(8,128)(2,1)S(1)}, u32[]{:S(2)}, u32[]{:S(2)}) %collective-permute-start.2) | collective-permute-done | bytes 69664 | tf_op jit(solution)/shard_map/ppermute | solution.py:516
  11.4 0.5 %collective-permute-start.4 = (bf16[272,128]{1,0:T(8,128)(2,1)S(1)}, bf16[272,128]{1,0:T(8,128)(2,1)S(1)}, u32[]{:S(2)}, u32[]{:S(2)}) collective-permute-start(bf16[272,128]{1,0:T(8,128)(2,1)S(1)} %collective-permute-done.2.refs_1_.above_ref.refs_11_), channel_id=1, source_target_pairs={{0,4},{4,0},{8,12},{12,8},{16,20},{20,16},{24,28},{28,24},{1,5},{5... | collective-permute-start | bytes 208904 | tf_op jit(solution)/shard_map/ppermute | solution.py:521
  11.9 2.1 %collective-permute-start.7 = (bf16[48,128]{1,0:T(8,128)(2,1)S(1)}, bf16[48,128]{1,0:T(8,128)(2,1)S(1)}, u32[]{:S(2)}, u32[]{:S(2)}) collective-permute-start(bf16[48,128]{1,0:T(8,128)(2,1)S(1)} %copy-done.7), channel_id=1, source_target_pairs={{0,28},{4,8},{8,4},{12,16},{16,12},{20,24},{24,20},{28,0},{1,29},{... | collective-permute-start | bytes 36872 | tf_op jit(solution)/shard_map/ppermute | solution.py:554
  13.9 1.0 %collective-permute-done.5.refs_0_.refs_10_ = bf16[272,128]{1,0:T(8,128)(2,1)S(1)} collective-permute-done((bf16[272,128]{1,0:T(8,128)(2,1)}, bf16[272,128]{1,0:T(8,128)(2,1)S(1)}, u32[]{:S(2)}, u32[]{:S(2)}) %collective-permute-start.5) | collective-permute-done | bytes 69664 | tf_op jit(solution)/shard_map/ppermute | solution.py:516
  14.9 0.9 %shard_map.129 = (f32[256,128]{1,0:T(8,128)S(1)}, f32[256,128]{1,0:T(8,128)S(1)}, f32[256,128]{1,0:T(8,128)S(1)}, f32[256,128]{1,0:T(8,128)S(1)}, f32[256,128]{1...) custom-call(bf16[16,256]{1,0:T(8,128)(2,1)S(1)} %concatenate.3.k_ref, ...), custom_call_target="tpu_custom_call" | custom-call | flops 4000000000 | bytes 4000000 | tf_op jit(solution)/shard_map/pallas_call | solution.py:154
  16.2 0.6 %shard_map.130 = (f32[256,128]{1,0:T(8,128)S(1)}, f32[256,128]{1,0:T(8,128)S(1)}, f32[256,128]{1,0:T(8,128)S(1)}, f32[256,128]{1,0:T(8,128)S(1)}, f32[64,512]{1,...) custom-call(bf16[16,256]{1,0:T(8,128)(2,1)S(1)} %concatenate.3.k_ref, ...), custom_call_target="tpu_custom_call" | custom-call | flops 2000000000 | bytes 2000000 | tf_op jit(solution)/shard_map/pallas_call | solution.py:154
  16.8 1.6 %collective-permute-start.8 = (bf16[64,512]{1,0:T(8,128)(2,1)S(1)}, bf16[64,512]{1,0:T(8,128)(2,1)S(1)}, u32[]{:S(2)}, u32[]{:S(2)}) collective-permute-start(bf16[64,512]{1,0:T(8,128)(2,1)S(1)} %get-tuple-element.69), channel_id=1, source_target_pairs={{0,8},{4,12},{8,0},{12,4},{16,24},{20,28},{24,16},{28,20},{1,9},{5... | collective-permute-start | bytes 196616 | tf_op jit(solution)/shard_map/ppermute | solution.py:521
  18.4 1.5 %collective-permute-start.9 = (bf16[64,512]{1,0:T(8,128)(2,1)S(1)}, bf16[64,512]{1,0:T(8,128)(2,1)S(1)}, u32[]{:S(2)}, u32[]{:S(2)}) collective-permute-start(bf16[64,512]{1,0:T(8,128)(2,1)S(1)} %get-tuple-element.70), channel_id=1, source_target_pairs={{0,16},{4,20},{8,24},{12,28},{16,0},{20,4},{24,8},{28,12},{1,17},{... | collective-permute-start | bytes 196616 | tf_op jit(solution)/shard_map/ppermute | solution.py:521
  19.9 0.5 %collective-permute-start.10 = (bf16[64,512]{1,0:T(8,128)(2,1)S(1)}, bf16[64,512]{1,0:T(8,128)(2,1)S(1)}, u32[]{:S(2)}, u32[]{:S(2)}) collective-permute-start(bf16[64,512]{1,0:T(8,128)(2,1)S(1)} %get-tuple-element.71), channel_id=1, source_target_pairs={{0,24},{4,28},{8,16},{12,20},{16,8},{20,12},{24,0},{28,4},{1,25},{... | collective-permute-start | bytes 196616 | tf_op jit(solution)/shard_map/ppermute | solution.py:521
  20.5 2.3 %pairs.1 = (f32[192,128]{1,0:T(8,128)S(1)}, f32[8,256]{1,0:T(8,128)S(1)}, f32[144,128]{1,0:T(8,128)S(1)}, bf16[48,512]{1,0:T(8,128)(2,1)S(1)}) custom-call(f32[8,128]{1,0:T(8,128)S(1)} %iota.10.where_ref, bf16[272,128]{1,0:T(8,128)(2,1)S(1)} %copy-done.1, bf16[272,128]{1,0:T(8,128)(2,1)S(1)} %collective-permute-done.refs_1_.flip_ref.refs_8_, ...), custom_call_target="tpu_custom_call" | custom-call | flops 4000000000 | bytes 1000000 | tf_op jit(solution)/shard_map/pairs/pallas_call | solution.py:461
  22.8 2.2 %collective-permute-done.10.refs_2_ = bf16[64,512]{1,0:T(8,128)(2,1)S(1)} collective-permute-done((bf16[64,512]{1,0:T(8,128)(2,1)S(1)}, bf16[64,512]{1,0:T(8,128)(2,1)S(1)}, u32[]{:S(2)}, u32[]{:S(2)}) %collective-permute-start.10) | collective-permute-done | bytes 65568 | tf_op jit(solution)/shard_map/ppermute | solution.py:521
  25.1 0.6 %collective-permute-start.11 = (bf16[112,512]{1,0:T(8,128)(2,1)S(1)}, bf16[112,512]{1,0:T(8,128)(2,1)S(1)}, u32[]{:S(2)}, u32[]{:S(2)}) collective-permute-start(bf16[112,512]{1,0:T(8,128)(2,1)S(1)} %get-tuple-element.74.refs_12_), channel_id=1, source_target_pairs={{0,8},{4,12},{8,0},{12,4},{16,24},{20,28},{24,16},{28,20},{1,9},{5... | collective-permute-start | bytes 344072 | tf_op jit(solution)/shard_map/ppermute | solution.py:521
  25.7 0.5 %collective-permute-start.12 = (bf16[112,512]{1,0:T(8,128)(2,1)S(1)}, bf16[112,512]{1,0:T(8,128)(2,1)S(1)}, u32[]{:S(2)}, u32[]{:S(2)}) collective-permute-start(bf16[112,512]{1,0:T(8,128)(2,1)S(1)} %get-tuple-element.74.refs_12_), channel_id=1, source_target_pairs={{0,16},{4,20},{8,24},{12,28},{16,0},{20,4},{24,8},{28,12},{1,17},{... | collective-permute-start | bytes 344072 | tf_op jit(solution)/shard_map/ppermute | solution.py:521
  26.2 2.4 %collective-permute-start.13 = (bf16[112,512]{1,0:T(8,128)(2,1)S(1)}, bf16[112,512]{1,0:T(8,128)(2,1)S(1)}, u32[]{:S(2)}, u32[]{:S(2)}) collective-permute-start(bf16[112,512]{1,0:T(8,128)(2,1)S(1)} %get-tuple-element.74.refs_12_), channel_id=1, source_target_pairs={{0,24},{4,28},{8,16},{12,20},{16,8},{20,12},{24,0},{28,4},{1,25},{... | collective-permute-start | bytes 344072 | tf_op jit(solution)/shard_map/ppermute | solution.py:521
  28.7 1.5 %collective-permute-done.11.refs_13_ = bf16[112,512]{1,0:T(8,128)(2,1)S(1)} collective-permute-done((bf16[112,512]{1,0:T(8,128)(2,1)S(1)}, bf16[112,512]{1,0:T(8,128)(2,1)S(1)}, u32[]{:S(2)}, u32[]{:S(2)}) %collective-permute-start.11) | collective-permute-done | bytes 114720 | tf_op jit(solution)/shard_map/ppermute | solution.py:521
  30.2 1.9 %collective-permute-done.12.refs_14_ = bf16[112,512]{1,0:T(8,128)(2,1)S(1)} collective-permute-done((bf16[112,512]{1,0:T(8,128)(2,1)S(1)}, bf16[112,512]{1,0:T(8,128)(2,1)S(1)}, u32[]{:S(2)}, u32[]{:S(2)}) %collective-permute-start.12) | collective-permute-done | bytes 114720 | tf_op jit(solution)/shard_map/ppermute | solution.py:521
  32.1 0.7 %shard_map.132.there_ref = f32[688,128]{1,0:T(8,128)S(1)} custom-call(f32[8,128]{1,0:T(8,128)S(1)} %iota.10.where_ref, bf16[16,256]{1,0:T(8,128)(2,1)S(1)} %concatenate.3.k_ref, f32[256,128]{1,0:T(8,128)S(1)} %get-tuple-element.77.refs_0_, f32[256,128]{1,0:T(8,128)S(1)} %get-tuple-element.78.refs_1_, f32[256,128]{1,0:T(8,128)S(1)} %get-tuple-element.79.refs_2_, ...), custom_call_target="tpu_custom_call" | custom-call | flops 3000000000 | bytes 4000000 | tf_op jit(solution)/shard_map/pallas_call | solution.py:328
  32.8 0.7 %shard_map.131.here_ref = f32[544,128]{1,0:T(8,128)S(1)} custom-call(bf16[16,256]{1,0:T(8,128)(2,1)S(1)} %concatenate.3.k_ref, f32[256,128]{1,0:T(8,128)S(1)} %get-tuple-element.51.refs_0_, f32[256,128]{1,0:T(8,128)S(1)} %get-tuple-element.57.refs_1_, f32[256,128]{1,0:T(8,128)S(1)} %get-tuple-element.59.refs_2_, f32[256,128]{1,0:T(8,128)S(1)} %get-tuple-element.60.refs_3_, ...), custom_call_target="tpu_custom_call" | custom-call | flops 3000000000 | bytes 4000000 | tf_op jit(solution)/shard_map/pallas_call | solution.py:328
  33.5 1.0 %collective-permute-done.14.sent_ref = f32[688,128]{1,0:T(8,128)S(1)} collective-permute-done((f32[688,128]{1,0:T(8,128)S(1)}, f32[688,128]{1,0:T(8,128)S(1)}, u32[]{:S(2)}, u32[]{:S(2)}) %collective-permute-start.14) | collective-permute-done | bytes 352288 | tf_op jit(solution)/shard_map/ppermute | solution.py:521
  34.5 0.8 %collective-permute-start.15 = (bf16[280,128]{1,0:T(8,128)(2,1)S(1)}, bf16[280,128]{1,0:T(8,128)(2,1)S(1)}, u32[]{:S(2)}, u32[]{:S(2)}) collective-permute-start(bf16[280,128]{1,0:T(8,128)(2,1)S(1)} %get-tuple-element.88), channel_id=1, source_target_pairs={{2,0},{3,1},{0,2},{1,3},{6,4},{7,5},{4,6},{5,7},{10,8},{11,9},{8,1... | collective-permute-start | bytes 215048 | tf_op jit(solution)/shard_map/ppermute | solution.py:516
  35.3 3.2 %collective-permute-start.16 = (bf16[280,128]{1,0:T(8,128)(2,1)S(1)}, bf16[280,128]{1,0:T(8,128)(2,1)S(1)}, u32[]{:S(2)}, u32[]{:S(2)}) collective-permute-start(bf16[280,128]{1,0:T(8,128)(2,1)S(1)} %get-tuple-element.89), channel_id=1, source_target_pairs={{1,0},{2,1},{3,2},{0,3},{5,4},{6,5},{7,6},{4,7},{9,8},{10,9},{11,1... | collective-permute-start | bytes 215048 | tf_op jit(solution)/shard_map/ppermute | solution.py:516
  38.4 3.4 %collective-permute-done.15.refs_0_ = bf16[280,128]{1,0:T(8,128)(2,1)S(1)} collective-permute-done((bf16[280,128]{1,0:T(8,128)(2,1)S(1)}, bf16[280,128]{1,0:T(8,128)(2,1)S(1)}, u32[]{:S(2)}, u32[]{:S(2)}) %collective-permute-start.15) | collective-permute-done | bytes 71712 | tf_op jit(solution)/shard_map/ppermute | solution.py:516
  41.9 2.7 %collective-permute-done.17.refs_2_ = bf16[280,128]{1,0:T(8,128)(2,1)S(1)} collective-permute-done((bf16[280,128]{1,0:T(8,128)(2,1)S(1)}, bf16[280,128]{1,0:T(8,128)(2,1)S(1)}, u32[]{:S(2)}, u32[]{:S(2)}) %collective-permute-start.17) | collective-permute-done | bytes 71712 | tf_op jit(solution)/shard_map/ppermute | solution.py:516
  44.6 0.7 %finish.1 = (f32[128,128]{1,0:T(8,128)}, f32[3,128]{1,0:T(4,128)}, f32[64,128]{1,0:T(8,128)}, f32[16,128]{1,0:T(8,128)}, f32[128,128]{1,0:T(8,128)}) custom-call(f32[280,128]{1,0:T(8,128)S(1)} %get-tuple-element.86.own_ref, f32[64,512]{1,0:T(8,128)S(1)} %get-tuple-element.87.total_ref, bf16[280,128]{1,0:T(8,128)(2,1)S(1)} %collective-permute-done.15.refs_0_, ...), custom_call_target="tpu_custom_call" | custom-call | tf_op jit(solution)/shard_map/finish/pallas_call | solution.py:500
  (42 shorter events, 1.1 us)
Async XLA Ops:
  0.6 8.1 %copy-start = (f32[2048,128]{1,0:T(8,128)S(1)}, f32[2048,128]{1,0:T(8,128)}, u32[]{:S(2)}) copy-start(f32[2048,128]{1,0:T(8,128)} %param.15) | copy-start | bytes 3145732
  2.2 6.2 %copy-start.6 = (s32[3,2048]{1,0:T(4,128)S(1)}, s32[3,2048]{1,0:T(4,128)}, u32[]{:S(2)}) copy-start(s32[3,2048]{1,0:T(4,128)} %param.14) | copy-start | bytes 73732
  2.2 6.7 %collective-permute-start = (bf16[272,128]{1,0:T(8,128)(2,1)}, bf16[272,128]{1,0:T(8,128)(2,1)S(1)}, u32[]{:S(2)}, u32[]{:S(2)}) collective-permute-start(bf16[272,128]{1,0:T(8,128)(2,1)} %get-tuple-element.50.refs_0_.own_ref.refs_8_), channel_id=1, source_target_pairs={{0,4},{4,0},{8,12},{12,8},{16,20},{20,16},{24,28},{28,24},{1,5},{5... | collective-permute-start | bytes 208904 | tf_op jit(solution)/shard_map/ppermute | solution.py:521
  2.8 7.8 %collective-permute-start.1 = (bf16[272,128]{1,0:T(8,128)(2,1)}, bf16[272,128]{1,0:T(8,128)(2,1)S(1)}, u32[]{:S(2)}, u32[]{:S(2)}) collective-permute-start(bf16[272,128]{1,0:T(8,128)(2,1)} %get-tuple-element.50.refs_0_.own_ref.refs_8_), channel_id=1, source_target_pairs={{3,0},{0,1},{1,2},{2,3},{7,4},{4,5},{5,6},{6,7},{11,8},{8,9},{9,10... | collective-permute-start | bytes 208904 | tf_op jit(solution)/shard_map/ppermute | solution.py:516
  5.4 6.0 %collective-permute-start.2 = (bf16[272,128]{1,0:T(8,128)(2,1)}, bf16[272,128]{1,0:T(8,128)(2,1)S(1)}, u32[]{:S(2)}, u32[]{:S(2)}) collective-permute-start(bf16[272,128]{1,0:T(8,128)(2,1)} %get-tuple-element.50.refs_0_.own_ref.refs_8_), channel_id=1, source_target_pairs={{1,0},{2,1},{3,2},{0,3},{5,4},{6,5},{7,6},{4,7},{9,8},{10,9},{11,1... | collective-permute-start | bytes 208904 | tf_op jit(solution)/shard_map/ppermute | solution.py:516
  7.5 7.4 %collective-permute-start.5 = (bf16[272,128]{1,0:T(8,128)(2,1)}, bf16[272,128]{1,0:T(8,128)(2,1)S(1)}, u32[]{:S(2)}, u32[]{:S(2)}) collective-permute-start(bf16[272,128]{1,0:T(8,128)(2,1)} %get-tuple-element.50.refs_0_.own_ref.refs_8_), channel_id=1, source_target_pairs={{2,0},{3,1},{0,2},{1,3},{6,4},{7,5},{4,6},{5,7},{10,8},{11,9},{8,1... | collective-permute-start | bytes 208904 | tf_op jit(solution)/shard_map/ppermute | solution.py:516
  8.6 0.9 %copy-start.1 = (bf16[272,128]{1,0:T(8,128)(2,1)S(1)}, bf16[272,128]{1,0:T(8,128)(2,1)}, u32[]{:S(2)}) copy-start(bf16[272,128]{1,0:T(8,128)(2,1)} %get-tuple-element.50.refs_0_.own_ref.refs_8_) | copy-start | bytes 208900
  8.9 3.0 %copy-start.7 = (bf16[48,128]{1,0:T(8,128)(2,1)S(1)}, bf16[48,128]{1,0:T(8,128)(2,1)}, u32[]{:S(2)}) copy-start(bf16[48,128]{1,0:T(8,128)(2,1)} %get-tuple-element.68) | copy-start | bytes 36868
  11.3 3.6 %collective-permute-start.3 = (bf16[272,128]{1,0:T(8,128)(2,1)S(1)}, bf16[272,128]{1,0:T(8,128)(2,1)S(1)}, u32[]{:S(2)}, u32[]{:S(2)}) collective-permute-start(bf16[272,128]{1,0:T(8,128)(2,1)S(1)} %collective-permute-done.1.refs_0_.below_ref.refs_9_), channel_id=1, source_target_pairs={{0,4},{4,0},{8,12},{12,8},{16,20},{20,16},{24,28},{28,24},{1,5},{5... | collective-permute-start | bytes 208904 | tf_op jit(solution)/shard_map/ppermute | solution.py:521
  11.4 3.6 %collective-permute-start.4 = (bf16[272,128]{1,0:T(8,128)(2,1)S(1)}, bf16[272,128]{1,0:T(8,128)(2,1)S(1)}, u32[]{:S(2)}, u32[]{:S(2)}) collective-permute-start(bf16[272,128]{1,0:T(8,128)(2,1)S(1)} %collective-permute-done.2.refs_1_.above_ref.refs_11_), channel_id=1, source_target_pairs={{0,4},{4,0},{8,12},{12,8},{16,20},{20,16},{24,28},{28,24},{1,5},{5... | collective-permute-start | bytes 208904 | tf_op jit(solution)/shard_map/ppermute | solution.py:521
  11.9 8.5 %collective-permute-start.7 = (bf16[48,128]{1,0:T(8,128)(2,1)S(1)}, bf16[48,128]{1,0:T(8,128)(2,1)S(1)}, u32[]{:S(2)}, u32[]{:S(2)}) collective-permute-start(bf16[48,128]{1,0:T(8,128)(2,1)S(1)} %copy-done.7), channel_id=1, source_target_pairs={{0,28},{4,8},{8,4},{12,16},{16,12},{20,24},{24,20},{28,0},{1,29},{... | collective-permute-start | bytes 36872 | tf_op jit(solution)/shard_map/ppermute | solution.py:554
  14.9 1.3 %collective-permute-start.6 = (bf16[272,128]{1,0:T(8,128)(2,1)S(1)}, bf16[272,128]{1,0:T(8,128)(2,1)S(1)}, u32[]{:S(2)}, u32[]{:S(2)}) collective-permute-start(bf16[272,128]{1,0:T(8,128)(2,1)S(1)} %collective-permute-done.5.refs_0_.refs_10_), channel_id=1, source_target_pairs={{0,4},{4,0},{8,12},{12,8},{16,20},{20,16},{24,28},{28,24},{1,5},{5... | collective-permute-start | bytes 208904 | tf_op jit(solution)/shard_map/ppermute | solution.py:521
  16.2 4.2 %copy-start.2 = (bf16[128,128]{1,0:T(8,128)(2,1)S(1)}, bf16[128,128]{1,0:T(8,128)(2,1)}, u32[]{:S(2)}) copy-start(bf16[128,128]{1,0:T(8,128)(2,1)} %wo_ref.1) | copy-start | bytes 98308
  16.2 4.2 %copy-start.3 = (s32[16,128]{1,0:T(8,128)S(1)}, s32[16,128]{1,0:T(8,128)}, u32[]{:S(2)}) copy-start(s32[16,128]{1,0:T(8,128)} %nbr_ref.1) | copy-start | bytes 24580
  16.8 3.6 %copy-start.4 = (bf16[16,128]{1,0:T(8,128)(2,1)S(1)}, bf16[16,128]{1,0:T(8,128)(2,1)}, u32[]{:S(2)}) copy-start(bf16[16,128]{1,0:T(8,128)(2,1)} %wr_ref.1) | copy-start | bytes 12292
  16.8 6.0 %collective-permute-start.8 = (bf16[64,512]{1,0:T(8,128)(2,1)S(1)}, bf16[64,512]{1,0:T(8,128)(2,1)S(1)}, u32[]{:S(2)}, u32[]{:S(2)}) collective-permute-start(bf16[64,512]{1,0:T(8,128)(2,1)S(1)} %get-tuple-element.69), channel_id=1, source_target_pairs={{0,8},{4,12},{8,0},{12,4},{16,24},{20,28},{24,16},{28,20},{1,9},{5... | collective-permute-start | bytes 196616 | tf_op jit(solution)/shard_map/ppermute | solution.py:521
  18.4 4.4 %collective-permute-start.9 = (bf16[64,512]{1,0:T(8,128)(2,1)S(1)}, bf16[64,512]{1,0:T(8,128)(2,1)S(1)}, u32[]{:S(2)}, u32[]{:S(2)}) collective-permute-start(bf16[64,512]{1,0:T(8,128)(2,1)S(1)} %get-tuple-element.70), channel_id=1, source_target_pairs={{0,16},{4,20},{8,24},{12,28},{16,0},{20,4},{24,8},{28,12},{1,17},{... | collective-permute-start | bytes 196616 | tf_op jit(solution)/shard_map/ppermute | solution.py:521
  19.9 0.7 %copy-start.5 = (s32[128]{0:T(128)S(1)}, s32[128]{0:T(128)}, u32[]{:S(2)}) copy-start(s32[128]{0:T(128)} %param.13) | copy-start | bytes 1540
  19.9 5.2 %collective-permute-start.10 = (bf16[64,512]{1,0:T(8,128)(2,1)S(1)}, bf16[64,512]{1,0:T(8,128)(2,1)S(1)}, u32[]{:S(2)}, u32[]{:S(2)}) collective-permute-start(bf16[64,512]{1,0:T(8,128)(2,1)S(1)} %get-tuple-element.71), channel_id=1, source_target_pairs={{0,24},{4,28},{8,16},{12,20},{16,8},{20,12},{24,0},{28,4},{1,25},{... | collective-permute-start | bytes 196616 | tf_op jit(solution)/shard_map/ppermute | solution.py:521
  25.1 5.1 %collective-permute-start.11 = (bf16[112,512]{1,0:T(8,128)(2,1)S(1)}, bf16[112,512]{1,0:T(8,128)(2,1)S(1)}, u32[]{:S(2)}, u32[]{:S(2)}) collective-permute-start(bf16[112,512]{1,0:T(8,128)(2,1)S(1)} %get-tuple-element.74.refs_12_), channel_id=1, source_target_pairs={{0,8},{4,12},{8,0},{12,4},{16,24},{20,28},{24,16},{28,20},{1,9},{5... | collective-permute-start | bytes 344072 | tf_op jit(solution)/shard_map/ppermute | solution.py:521
  25.7 6.4 %collective-permute-start.12 = (bf16[112,512]{1,0:T(8,128)(2,1)S(1)}, bf16[112,512]{1,0:T(8,128)(2,1)S(1)}, u32[]{:S(2)}, u32[]{:S(2)}) collective-permute-start(bf16[112,512]{1,0:T(8,128)(2,1)S(1)} %get-tuple-element.74.refs_12_), channel_id=1, source_target_pairs={{0,16},{4,20},{8,24},{12,28},{16,0},{20,4},{24,8},{28,12},{1,17},{... | collective-permute-start | bytes 344072 | tf_op jit(solution)/shard_map/ppermute | solution.py:521
  26.2 5.9 %collective-permute-start.13 = (bf16[112,512]{1,0:T(8,128)(2,1)S(1)}, bf16[112,512]{1,0:T(8,128)(2,1)S(1)}, u32[]{:S(2)}, u32[]{:S(2)}) collective-permute-start(bf16[112,512]{1,0:T(8,128)(2,1)S(1)} %get-tuple-element.74.refs_12_), channel_id=1, source_target_pairs={{0,24},{4,28},{8,16},{12,20},{16,8},{20,12},{24,0},{28,4},{1,25},{... | collective-permute-start | bytes 344072 | tf_op jit(solution)/shard_map/ppermute | solution.py:521
  32.8 1.7 %collective-permute-start.14 = (f32[688,128]{1,0:T(8,128)S(1)}, f32[688,128]{1,0:T(8,128)S(1)}, u32[]{:S(2)}, u32[]{:S(2)}) collective-permute-start(f32[688,128]{1,0:T(8,128)S(1)} %shard_map.132.there_ref), channel_id=1, source_target_pairs={{0,4},{4,0},{8,12},{12,8},{16,20},{20,16},{24,28},{28,24},{1,5},{5... | collective-permute-start | bytes 1056776 | tf_op jit(solution)/shard_map/ppermute | solution.py:521
  34.5 7.4 %collective-permute-start.15 = (bf16[280,128]{1,0:T(8,128)(2,1)S(1)}, bf16[280,128]{1,0:T(8,128)(2,1)S(1)}, u32[]{:S(2)}, u32[]{:S(2)}) collective-permute-start(bf16[280,128]{1,0:T(8,128)(2,1)S(1)} %get-tuple-element.88), channel_id=1, source_target_pairs={{2,0},{3,1},{0,2},{1,3},{6,4},{7,5},{4,6},{5,7},{10,8},{11,9},{8,1... | collective-permute-start | bytes 215048 | tf_op jit(solution)/shard_map/ppermute | solution.py:516
  35.3 6.6 %collective-permute-start.16 = (bf16[280,128]{1,0:T(8,128)(2,1)S(1)}, bf16[280,128]{1,0:T(8,128)(2,1)S(1)}, u32[]{:S(2)}, u32[]{:S(2)}) collective-permute-start(bf16[280,128]{1,0:T(8,128)(2,1)S(1)} %get-tuple-element.89), channel_id=1, source_target_pairs={{1,0},{2,1},{3,2},{0,3},{5,4},{6,5},{7,6},{4,7},{9,8},{10,9},{11,1... | collective-permute-start | bytes 215048 | tf_op jit(solution)/shard_map/ppermute | solution.py:516
  38.4 6.1 %collective-permute-start.17 = (bf16[280,128]{1,0:T(8,128)(2,1)S(1)}, bf16[280,128]{1,0:T(8,128)(2,1)S(1)}, u32[]{:S(2)}, u32[]{:S(2)}) collective-permute-start(bf16[280,128]{1,0:T(8,128)(2,1)S(1)} %get-tuple-element.90), channel_id=1, source_target_pairs={{3,0},{0,1},{1,2},{2,3},{7,4},{4,5},{5,6},{6,7},{11,8},{8,9},{9,10... | collective-permute-start | bytes 215048 | tf_op jit(solution)/shard_map/ppermute | solution.py:516
